TPU v7x, 512 devices: a whole 4x8x8 slice. The times are simulated.
512 devices in a mesh: depth: 16 (over z, y_lo), rows: 32 (over x, y_hi, core).
Axes of the slice: x: 4, y: 8 (y_hi: 4, y_lo: 2; y = y_hi * 2 + y_lo), z: 8, core: 2. Of those that a mesh axis runs over, the one named last changes fastest.
Arguments:
- target: float32 [16, 2, 4096, 4096], P('depth', None, 'rows'), may hold values from -6 to 6
- depth_index: int32 [16], P('depth'), may hold values from 0 to 255
- band_mask: int32 [16, 2, 4096], P('depth'), may hold values from 0 to 1, as said below
Outputs:
- hologram: float32 [2, 4096, 4096], P(None, ('depth', 'rows'))
Inputs may be any that keep to these rules, and one draw needn't show every extreme that they name: `band_mask`: for each plane and each of the two dimensions, the ones are exactly the frequency indices k with min(k, 4096 - k) below a cutoff between 512 and 2048.
All inputs are finite; a program needn't handle non-finite values.
Results may differ from a plain program's by a relative error of at most 0.0009.
Values sent between devices are 32-bit elements; how exact they have to be, the bound alone decides.
A program may use at most 64 MiB of HBM per device.

v0:
```python
import functools
import math

import jax
import jax.numpy as jnp
import ml_dtypes
import numpy as np
from jax import lax
from jax.experimental import pallas as pl
from jax.experimental.pallas import tpu as pltpu
from jax.sharding import PartitionSpec as P

MESH = pl.DeviceIdType.MESH
N = 4096
LOW = 32
HIGH = 128
Z = 8
CHUNKS = 4
CW = HIGH // CHUNKS
CT = CW // 8
F32 = jnp.float32
BF16 = jnp.bfloat16


def tables():
    angle = 2.0 * np.pi / N * np.outer(np.arange(LOW), np.arange(HIGH))
    turn = np.stack([np.cos(angle), np.sin(angle)]) / 64.0
    turn = np.broadcast_to(turn[:, :, None, :], (2, LOW, 8, HIGH)).astype(np.float32)
    angle = 2.0 * np.pi / LOW * np.outer(np.arange(1, 4), np.arange(8))
    small = np.stack([np.cos(angle), np.sin(angle)])
    small = np.broadcast_to(small[:, :, :, None, None], (2, 3, 8, 8, HIGH)).astype(np.float32)
    angle = 2.0 * np.pi / HIGH * (np.outer(np.arange(HIGH), np.arange(HIGH)) % HIGH)
    cosine, sine = np.cos(angle), np.sin(angle)
    ahead = np.block([[cosine, -sine], [sine, cosine]])
    parts = []
    for matrix in (ahead, ahead.T):
        top = matrix.astype(np.float32).astype(ml_dtypes.bfloat16)
        rest = (matrix - top.astype(np.float64)).astype(np.float32).astype(ml_dtypes.bfloat16)
        parts += [top, rest]
    return turn, small, np.stack(parts)


def dft4(a, sign):
    (r0, i0), (r1, i1), (r2, i2), (r3, i3) = a
    s0r, s0i, d0r, d0i = r0 + r2, i0 + i2, r0 - r2, i0 - i2
    s1r, s1i, d1r, d1i = r1 + r3, i1 + i3, r1 - r3, i1 - i3
    up, down = (d0r - d1i, d0i + d1r), (d0r + d1i, d0i - d1r)
    first, third = (up, down) if sign > 0 else (down, up)
    return [(s0r + s1r, s0i + s1i), first, (s0r - s1r, s0i - s1i), third]


def dft32(re, im, small_ref, sign):
    half = math.sqrt(0.5)
    columns = dft4([(re[8 * n : 8 * n + 8], im[8 * n : 8 * n + 8]) for n in range(4)], sign)
    turned = [columns[0]]
    for k in range(1, 4):
        r, i = columns[k]
        c, s = small_ref[0, k - 1], small_ref[1, k - 1]
        turned.append((r * c + i * s, i * c - r * s) if sign < 0 else (r * c - i * s, i * c + r * s))
    re = jnp.stack([t[0] for t in turned])
    im = jnp.stack([t[1] for t in turned])
    rows = [(re[:, n], im[:, n]) for n in range(8)]
    even = dft4(rows[0::2], sign)
    odd = dft4(rows[1::2], sign)
    (r1, i1), (r2, i2), (r3, i3) = odd[1:]
    if sign < 0:
        odd = [odd[0], ((r1 + i1) * half, (i1 - r1) * half), (i2, -r2), ((i3 - r3) * half, (-r3 - i3) * half)]
    else:
        odd = [odd[0], ((r1 - i1) * half, (i1 + r1) * half), (-i2, r2), ((-r3 - i3) * half, (r3 - i3) * half)]
    result = [(e[0] + o[0], e[1] + o[1]) for e, o in zip(even, odd)]
    return result + [(e[0] - o[0], e[1] - o[1]) for e, o in zip(even, odd)]


def joined(pieces):
    return jnp.concatenate([p[0] for p in pieces]), jnp.concatenate([p[1] for p in pieces])


def split_dot(left, w_ref, which):
    top = left.astype(BF16)
    rest = (left - top.astype(F32)).astype(BF16)
    w_top, w_rest = w_ref[which], w_ref[which + 1]
    dot = functools.partial(jnp.dot, preferred_element_type=F32)
    return dot(top, w_top) + (dot(rest, w_top) + dot(top, w_rest))


def along_lanes(re, im, w_ref, which):
    left = jnp.concatenate([re.reshape(8 * LOW, HIGH), im.reshape(8 * LOW, HIGH)], axis=1)
    result = split_dot(left, w_ref, which)
    return result[:, :HIGH].reshape(LOW, 8, HIGH), result[:, HIGH:].reshape(LOW, 8, HIGH)


def kernel(
    x_ref, mask_ref, level_ref, turn_ref, small_ref, w_ref, out_ref,
    xbuf, tbuf, send, recv, prop, part, ring, own, pair, final, final_in, mask_in, level_in,
    x_sem, send_sem, recv_sem, ring_send, ring_recv, pair_send, pair_recv, final_send, final_recv, par_send, par_recv,
):
    depth = lax.axis_index("depth")
    row = lax.axis_index("rows")
    z, y_lo = depth // 2, lax.rem(depth, 2)
    core, y_hi, x = lax.rem(row, 2), lax.rem(row // 2, 4), row // 8
    other = depth + 1 - 2 * y_lo
    up, down = lax.rem(depth + 2, 2 * Z), lax.rem(depth + 2 * Z - 2, 2 * Z)

    def peer(i):
        h = lax.rem(i, 4)
        to_y = lax.rem(y_hi + lax.rem(h, 2) * 2 + h // 2, 4)
        to_core = lax.rem(core + lax.rem(i // 4, 2), 2)
        to_x = lax.rem(x + i // 8, 4)
        return (to_x * 4 + to_y) * 2 + to_core

    def load(a):
        return pltpu.make_async_copy(x_ref.at[0, :, :, pl.ds(pl.multiple_of(a * HIGH, HIGH), HIGH)], xbuf.at[a], x_sem)

    lax.fori_loop(0, LOW, lambda a, c: (load(a).start(), c)[1], 0)

    barrier = pltpu.get_barrier_semaphore()

    def greet(i, c):
        pl.semaphore_signal(barrier, inc=1, device_id=(other, i), device_id_type=MESH)
        return c

    lax.fori_loop(0, 32, greet, 0)
    pl.semaphore_signal(barrier, inc=1, device_id=(up, row), device_id_type=MESH)
    pl.semaphore_signal(barrier, inc=1, device_id=(down, row), device_id_type=MESH)

    pltpu.make_async_copy(xbuf, xbuf, x_sem).wait()

    def width_first(t, c):
        rows = pl.ds(pl.multiple_of(t * 8, 8), 8)
        re, im = joined(dft32(xbuf[:, 0, rows, :], xbuf[:, 1, rows, :], small_ref, -1))
        cosine, sine = turn_ref[0], turn_ref[1]
        tbuf[:, 0, rows, :] = re * cosine + im * sine
        tbuf[:, 1, rows, :] = im * cosine - re * sine
        return c

    lax.fori_loop(0, 16, width_first, 0)

    pl.semaphore_wait(barrier, 34)

    mask_copy = pltpu.make_async_remote_copy(
        mask_ref, mask_in, par_send.at[0], par_recv.at[0], device_id=(other, row), device_id_type=MESH
    )
    level_copy = pltpu.make_async_remote_copy(
        level_ref, level_in, par_send.at[1], par_recv.at[1], device_id=(other, row), device_id_type=MESH
    )
    mask_copy.start()
    level_copy.start()

    def exchange(q, to):
        return pltpu.make_async_remote_copy(
            send.at[q, to], recv.at[q, row], send_sem.at[q], recv_sem.at[q], device_id=(other, to), device_id_type=MESH
        )

    def exchange_whole(q):
        return pltpu.make_async_remote_copy(
            send.at[q], recv.at[q], send_sem.at[q], recv_sem.at[q], device_id=(other, row), device_id_type=MESH
        )

    def width_last(g, c):
        @pl.when(g > 0)
        def _():
            for h in range(4):
                exchange(0, peer((g - 1) * 4 + h)).start()

        for h in range(4):
            to = peer(g * 4 + h)
            both = split_dot(jnp.concatenate([tbuf[to, 0], tbuf[to, 1]], axis=1), w_ref, 0)
            for k in range(2):
                turned = both[:, k * HIGH : (k + 1) * HIGH].T
                for q in range(CHUNKS):
                    send[q, to, k] = turned[q * CW : (q + 1) * CW]
        return c

    lax.fori_loop(0, 8, width_last, 0)
    lax.fori_loop(28, 32, lambda i, c: (exchange(0, peer(i)).start(), c)[1], 0)
    lax.fori_loop(0, 32, lambda i, c: (exchange(1, peer(i)).start(), c)[1], 0)

    mask_copy.wait()
    level_copy.wait()
    distance = 100.0 + 2.0 * level_in[...].astype(F32)

    def cutoff(k):
        total = jnp.sum(jnp.sum(mask_in[k].astype(F32), axis=1, keepdims=True), axis=0, keepdims=True)
        return jnp.broadcast_to((total + 1.0) * 0.5, (8, HIGH))[None]

    cut_y, cut_x = cutoff(0), cutoff(1)
    shape = (8, 8, HIGH)

    def signed(k):
        return jnp.where(k < N // 2, k, k - N).astype(F32)

    def propagate(i, c):
        t, g = i // 4, lax.rem(i, 4)
        k_y = signed(lax.broadcasted_iota(jnp.int32, shape, 0) + g * 8 + 32 * lax.broadcasted_iota(jnp.int32, shape, 2))
        k_x = signed(row + 32 * (t * 8 + lax.broadcasted_iota(jnp.int32, shape, 1)))
        f_y, f_x = k_y * (1.0 / N), k_x * (1.0 / N)
        square = f_y * f_y + f_x * f_x
        quarters = (-4.0 * distance[None]) * (square / (2.0 + jnp.sqrt(4.0 - square)))
        whole = jnp.floor(quarters + 0.5)
        v = (quarters - whole) * (0.5 * math.pi)
        quadrant = whole - 4.0 * jnp.floor(whole * 0.25)
        v2 = v * v
        sine = v + v * v2 * (-1.6666654611e-1 + v2 * (8.3321608736e-3 - v2 * 1.9515295891e-4))
        cosine = 1.0 - 0.5 * v2 + v2 * v2 * (4.166664568298827e-2 + v2 * (-1.388731625493765e-3 + v2 * 2.443315711809948e-5))
        odd = (quadrant == 1.0) | (quadrant == 3.0)
        re = jnp.where(odd, sine, cosine)
        im = jnp.where(odd, cosine, sine)
        inside = (jnp.abs(k_y) < cut_y) & (jnp.abs(k_x) < cut_x)
        weight = jnp.where(inside, 1.0, 0.0)
        prop[t, pl.ds(g * 8, 8), 0] = jnp.where((quadrant == 1.0) | (quadrant == 2.0), -re, re) * weight
        prop[t, pl.ds(g * 8, 8), 1] = jnp.where(quadrant >= 2.0, -im, im) * weight
        return c

    lax.fori_loop(0, 64, propagate, 0)

    def ring_copy(q, step, toward, source):
        return pltpu.make_async_remote_copy(
            part.at[q, pl.ds(source * 4, 4)], ring.at[q, step], ring_send.at[q, step], ring_recv.at[q, step],
            device_id=(toward, row), device_id_type=MESH,
        )

    def pair_copy(q):
        return pltpu.make_async_remote_copy(
            own.at[q, pl.ds(y_lo * 2, 2)], pair.at[q], pair_send.at[q], pair_recv.at[q],
            device_id=(other, row), device_id_type=MESH,
        )

    def chunk(q, c):
        exchange_whole(q).wait_recv()

        def tile(t, c):
            rows = pl.ds(pl.multiple_of(t * 8, 8), 8)
            re, im = joined(dft32(recv[q, :, 0, rows, :], recv[q, :, 1, rows, :], small_ref, -1))
            cosine, sine = turn_ref[0], turn_ref[1]
            re, im = along_lanes(re * cosine + im * sine, im * cosine - re * sine, w_ref, 0)
            p_re, p_im = prop[q * CT + t, :, 0], prop[q * CT + t, :, 1]
            re, im = along_lanes(re * p_re - im * p_im, re * p_im + im * p_re, w_ref, 2)
            re, im = joined(dft32(re * cosine - im * sine, im * cosine + re * sine, small_ref, 1))
            part[q, :, 0, rows, :] = re
            part[q, :, 1, rows, :] = im
            return c

        lax.fori_loop(0, CT, tile, 0)

        @pl.when(q < CHUNKS - 2)
        def _():
            lax.fori_loop(0, 32, lambda i, c: (exchange(q + 2, peer(i)).start(), c)[1], 0)

        ring_copy(q, 0, up, lax.rem(z + 4, Z)).start()
        ring_copy(q, 4, down, lax.rem(z + 5, Z)).start()
        for step in range(1, 4):
            source = lax.rem(z + 4 - step, Z)
            ring_copy(q, step - 1, up, source).wait_recv()
            part[q, pl.ds(source * 4, 4)] = part[q, pl.ds(source * 4, 4)] + ring[q, step - 1]
            if step < 3:
                back = lax.rem(z + 5 + step, Z)
                ring_copy(q, 3 + step, down, back).wait_recv()
                part[q, pl.ds(back * 4, 4)] = part[q, pl.ds(back * 4, 4)] + ring[q, 3 + step]
            ring_copy(q, step, up, source).start()
            if step < 3:
                ring_copy(q, 4 + step, down, back).start()
        ring_copy(q, 6, down, z).wait_recv()
        ring_copy(q, 3, up, z).wait_recv()
        own[q] = part[q, pl.ds(z * 4, 4)] + (ring[q, 3] + ring[q, 6])
        pair_copy(q).start()
        return c

    lax.fori_loop(0, CHUNKS, chunk, 0)

    for q in range(CHUNKS):
        pair_copy(q).wait_recv()
    keep = 2 - 2 * y_lo
    for half in range(2):
        for k in range(2):
            block = jnp.concatenate([own[q, keep + half, k] + pair[q, half, k] for q in range(CHUNKS)])
            final[half * 16 : half * 16 + 16, k] = block.T.reshape(16, 8, HIGH)

    def deliver(to):
        return pltpu.make_async_remote_copy(
            final.at[to], final_in.at[row], final_send, final_recv, device_id=(other, to), device_id_type=MESH
        )

    deliver_whole = pltpu.make_async_remote_copy(
        final, final_in, final_send, final_recv, device_id=(other, row), device_id_type=MESH
    )
    lax.fori_loop(0, 32, lambda i, c: (deliver(peer(i)).start(), c)[1], 0)

    def settle(q, c):
        exchange_whole(q).wait_send()
        pair_copy(q).wait_send()
        for step in range(7):
            ring_copy(q, step, up, z).wait_send()
        return c

    lax.fori_loop(0, CHUNKS, settle, 0)
    deliver_whole.wait_recv()

    re, im = along_lanes(final_in[:, 0], final_in[:, 1], w_ref, 2)
    cosine, sine = turn_ref[0] * 0.25, turn_ref[1] * 0.25
    pieces = dft32(re * cosine - im * sine, im * cosine + re * sine, small_ref, 1)
    for k in range(8):
        for j in range(4):
            lanes = pl.ds((k * 4 + j) * HIGH, HIGH)
            out_ref[0, :, lanes] = pieces[k][0][j]
            out_ref[1, :, lanes] = pieces[k][1][j]
    deliver_whole.wait_send()


def local(target, depth_index, band_mask):
    turn, small, matrices = tables()
    level = jnp.broadcast_to(depth_index.reshape(1, 1), (8, HIGH))
    vmem = pl.BlockSpec(memory_space=pltpu.VMEM)
    dma = pltpu.SemaphoreType.DMA
    return pl.pallas_call(
        kernel,
        out_shape=jax.ShapeDtypeStruct((2, 8, N), F32),
        in_specs=[pl.BlockSpec(memory_space=pl.ANY)] + [vmem] * 5,
        out_specs=vmem,
        scratch_shapes=[
            pltpu.VMEM((LOW, 2, HIGH, HIGH), F32),
            pltpu.VMEM((LOW, 2, HIGH, HIGH), F32),
            pltpu.VMEM((CHUNKS, LOW, 2, CW, HIGH), F32),
            pltpu.VMEM((CHUNKS, LOW, 2, CW, HIGH), F32),
            pltpu.VMEM((16, LOW, 2, 8, HIGH), F32),
            pltpu.VMEM((CHUNKS, LOW, 2, CW, HIGH), F32),
            pltpu.VMEM((CHUNKS, 7, 4, 2, CW, HIGH), F32),
            pltpu.VMEM((CHUNKS, 4, 2, CW, HIGH), F32),
            pltpu.VMEM((CHUNKS, 2, 2, CW, HIGH), F32),
            pltpu.VMEM((LOW, 2, 8, HIGH), F32),
            pltpu.VMEM((LOW, 2, 8, HIGH), F32),
            pltpu.VMEM((2, LOW, HIGH), jnp.int32),
            pltpu.VMEM((8, HIGH), jnp.int32),
            dma,
            dma((CHUNKS,)),
            dma((CHUNKS,)),
            dma((CHUNKS, 7)),
            dma((CHUNKS, 7)),
            dma((CHUNKS,)),
            dma((CHUNKS,)),
            dma,
            dma,
            dma((2,)),
            dma((2,)),
        ],
        compiler_params=pltpu.CompilerParams(
            collective_id=0, has_side_effects=True, vmem_limit_bytes=60 * 1024 * 1024
        ),
        name="hologram",
    )(target, band_mask.reshape(2, LOW, HIGH), level, turn, small, matrices)


def solution(mesh):
    in_specs = (P("depth", None, "rows", None), P("depth"), P("depth", None, None))
    out_specs = P(None, ("depth", "rows"), None)
    return jax.shard_map(local, mesh=mesh, in_specs=in_specs, out_specs=out_specs, check_vma=False)
```

profile of v0, /device:TPU:1, one launch (start us, length us, event | category | flops | bytes accessed | tf_op | source)
XLA Modules:
  0.0 154.3 jit_solution(17575331311417485184)
XLA Ops:
  0.7 0.6 broadcast_in_dim.8.level_ref
  1.2 1.4 copy.9
  2.6 150.0 %hologram.1 = f32[2,8,4096]{2,1,0:T(8,128)} custom-call(f32[1,2,128,4096]{3,2,1,0:T(8,128)} %x_ref.1, s32[2,32,128]{2,1,0:T(8,128)} %bitcast.7, s32[8,128]{1,0:T(8,128)} %broadcast_in_dim.8.level_ref, f32[2,32,8,128]{3,2,1,0:T(8,128)} %constant.6.clone.turn_ref, f32[2,3,8,8,128]{4,3,2,1,0:T(8,128)} %constant.7.clone.small_ref, ...), custom_call_target="tpu_custom_call" | custom-call | tf_op jit(solution)/shard_map/hologram/pallas_call | solution.py:314
  152.6 1.7 %copy.12 = f32[2,8,4096]{2,1,0:T(8,128)} copy(f32[2,8,4096]{2,1,0:T(8,128)} %hologram.1) | data formatting | bytes 524288
where the time goes:
time: 155 us; the launch traced here: 154 us
  Pallas kernels  150 us (97%)
  local copies, waits for them, and re-layouts  3.64 us (2%)
    pallas_call x1, Pallas kernels, local(): pl.pallas_call(kernel, out_shape=jax.ShapeDtypeStruct((2, 8, N), F32), in...  150 us

commit v1 on v0

v1 whole, which is shorter than its diff:
```python
import functools
import math

import jax
import jax.numpy as jnp
import ml_dtypes
import numpy as np
from jax import lax
from jax.experimental import pallas as pl
from jax.experimental.pallas import tpu as pltpu
from jax.sharding import PartitionSpec as P

MESH = pl.DeviceIdType.MESH
N = 4096
LOW = 32
HIGH = 128
Z = 8
TILES = 16
WIDE = 7
CHUNKS = WIDE + 2
F32 = jnp.float32
BF16 = jnp.bfloat16


def tables():
    angle = 2.0 * np.pi / N * np.outer(np.arange(LOW), np.arange(HIGH))
    turn = np.stack([np.cos(angle), np.sin(angle)]) / 64.0
    turn = np.broadcast_to(turn[:, :, None, :], (2, LOW, 8, HIGH)).astype(np.float32)
    angle = 2.0 * np.pi / LOW * np.outer(np.arange(1, 4), np.arange(8))
    small = np.stack([np.cos(angle), np.sin(angle)])
    small = np.broadcast_to(small[:, :, :, None, None], (2, 3, 8, 8, HIGH)).astype(np.float32)
    angle = 2.0 * np.pi / HIGH * (np.outer(np.arange(HIGH), np.arange(HIGH)) % HIGH)
    cosine, sine = np.cos(angle), np.sin(angle)
    ahead = np.block([[cosine, -sine], [sine, cosine]])
    parts = []
    for matrix in (ahead, ahead.T):
        top = matrix.astype(np.float32).astype(ml_dtypes.bfloat16)
        rest = (matrix - top.astype(np.float64)).astype(np.float32).astype(ml_dtypes.bfloat16)
        parts += [top, rest]
    order = np.arange(256).reshape(2, 2, 64).swapaxes(0, 1).reshape(256)
    parts += [parts[2][order], parts[3][order]]
    return turn, small, np.stack(parts)


def dft4(a, sign):
    (r0, i0), (r1, i1), (r2, i2), (r3, i3) = a
    s0r, s0i, d0r, d0i = r0 + r2, i0 + i2, r0 - r2, i0 - i2
    s1r, s1i, d1r, d1i = r1 + r3, i1 + i3, r1 - r3, i1 - i3
    up, down = (d0r - d1i, d0i + d1r), (d0r + d1i, d0i - d1r)
    first, third = (up, down) if sign > 0 else (down, up)
    return [(s0r + s1r, s0i + s1i), first, (s0r - s1r, s0i - s1i), third]


def dft32(re, im, small_ref, sign):
    half = math.sqrt(0.5)
    columns = dft4([(re[8 * n : 8 * n + 8], im[8 * n : 8 * n + 8]) for n in range(4)], sign)
    turned = [columns[0]]
    for k in range(1, 4):
        r, i = columns[k]
        c, s = small_ref[0, k - 1], small_ref[1, k - 1]
        turned.append((r * c + i * s, i * c - r * s) if sign < 0 else (r * c - i * s, i * c + r * s))
    re = jnp.stack([t[0] for t in turned])
    im = jnp.stack([t[1] for t in turned])
    rows = [(re[:, n], im[:, n]) for n in range(8)]
    even = dft4(rows[0::2], sign)
    odd = dft4(rows[1::2], sign)
    (r1, i1), (r2, i2), (r3, i3) = odd[1:]
    if sign < 0:
        odd = [odd[0], ((r1 + i1) * half, (i1 - r1) * half), (i2, -r2), ((i3 - r3) * half, (-r3 - i3) * half)]
    else:
        odd = [odd[0], ((r1 - i1) * half, (i1 + r1) * half), (-i2, r2), ((-r3 - i3) * half, (r3 - i3) * half)]
    result = [(e[0] + o[0], e[1] + o[1]) for e, o in zip(even, odd)]
    return result + [(e[0] - o[0], e[1] - o[1]) for e, o in zip(even, odd)]


def joined(pieces):
    return jnp.concatenate([p[0] for p in pieces]), jnp.concatenate([p[1] for p in pieces])


def split_dot(left, w_ref, which):
    top = left.astype(BF16)
    rest = (left - top.astype(F32)).astype(BF16)
    w_top, w_rest = w_ref[which], w_ref[which + 1]
    dot = functools.partial(jnp.dot, preferred_element_type=F32)
    return dot(top, w_top) + (dot(rest, w_top) + dot(top, w_rest))


def along_lanes(re, im, w_ref, which):
    left = jnp.concatenate([re.reshape(8 * LOW, HIGH), im.reshape(8 * LOW, HIGH)], axis=1)
    result = split_dot(left, w_ref, which)
    return result[:, :HIGH].reshape(LOW, 8, HIGH), result[:, HIGH:].reshape(LOW, 8, HIGH)


def kernel(
    x_ref, mask_ref, level_ref, turn_ref, small_ref, w_ref, out_ref,
    xbuf, tbuf, send, recv, prop, part, ring, own, pair, final, final_in, mask_in, level_at, level_out, level_in,
    turn, small, w,
    x_sem, in_sem, send_sem, recv_sem, ring_send, ring_recv, pair_send, pair_recv, final_send, final_recv,
    par_send, par_recv,
):
    depth = lax.axis_index("depth")
    row = lax.axis_index("rows")
    z, y_lo = depth // 2, lax.rem(depth, 2)
    core, y_hi, x = lax.rem(row, 2), lax.rem(row // 2, 4), row // 8
    other = depth + 1 - 2 * y_lo
    up, down = lax.rem(depth + 2, 2 * Z), lax.rem(depth + 2 * Z - 2, 2 * Z)

    def peer(i):
        h = lax.rem(i, 4)
        to_y = lax.rem(y_hi + lax.rem(h, 2) * 2 + h // 2, 4)
        to_core = lax.rem(core + lax.rem(i // 4, 2), 2)
        to_x = lax.rem(x + i // 8, 4)
        return (to_x * 4 + to_y) * 2 + to_core

    def load(g):
        rows = pl.ds(pl.multiple_of(g * 32, 32), 32)
        return pltpu.make_async_copy(x_ref.at[0, :, rows, :], xbuf.at[:, rows, :], x_sem.at[g])

    load_small = pltpu.make_async_copy(small_ref, small, in_sem.at[0])
    load_turn = pltpu.make_async_copy(turn_ref, turn, in_sem.at[1])
    load_w = pltpu.make_async_copy(w_ref, w, in_sem.at[2])
    load_level = pltpu.make_async_copy(level_ref, level_at, in_sem.at[3])
    load_small.start()
    load(0).start()
    load_turn.start()
    for g in range(1, 4):
        load(g).start()
    load_w.start()
    load_level.start()

    barrier = pltpu.get_barrier_semaphore()

    def greet(i, c):
        pl.semaphore_signal(barrier, inc=1, device_id=(other, i), device_id_type=MESH)
        return c

    lax.fori_loop(0, 32, greet, 0)
    pl.semaphore_signal(barrier, inc=1, device_id=(up, row), device_id_type=MESH)
    pl.semaphore_signal(barrier, inc=1, device_id=(down, row), device_id_type=MESH)

    load_small.wait()
    load_turn.wait()

    def width_first(t, c):
        rows = pl.ds(pl.multiple_of(t * 8, 8), 8)
        cells = [jnp.stack([xbuf[k, rows, a * HIGH : (a + 1) * HIGH] for a in range(LOW)]) for k in range(2)]
        re, im = joined(dft32(cells[0], cells[1], small, -1))
        cosine, sine = turn[0], turn[1]
        tbuf[:, 0, rows, :] = re * cosine + im * sine
        tbuf[:, 1, rows, :] = im * cosine - re * sine
        return c

    def width_group(g, c):
        load(g).wait()
        return lax.fori_loop(g * 4, g * 4 + 4, width_first, c)

    with jax.named_scope("A1"):
        lax.fori_loop(0, 4, width_group, 0)

    load_level.wait()
    level_out[...] = jnp.full((8, HIGH), level_at[0].astype(F32))
    load_w.wait()
    with jax.named_scope("barrier"):
        pl.semaphore_wait(barrier, 34)

    def exchange(q, t0, n, to):
        tiles = pl.ds(t0, n)
        return pltpu.make_async_remote_copy(
            send.at[tiles, to], recv.at[tiles, row], send_sem.at[q], recv_sem.at[q],
            device_id=(other, to), device_id_type=MESH,
        )

    def exchange_whole(q, t0, n):
        tiles = pl.ds(t0, n)
        return pltpu.make_async_remote_copy(
            send.at[tiles], recv.at[tiles], send_sem.at[q], recv_sem.at[q],
            device_id=(other, row), device_id_type=MESH,
        )

    def exchange_all(q, t0, n):
        def some(i, c):
            for h in range(4):
                exchange(q, t0, n, peer(i * 4 + h)).start()
            return c

        lax.fori_loop(0, 8, some, 0)

    def width_last(g, c):
        @pl.when(g > 0)
        def _():
            for h in range(4):
                exchange(0, 0, 2, peer((g - 1) * 4 + h)).start()

        for h in range(4):
            to = peer(g * 4 + h)
            both = split_dot(jnp.concatenate([tbuf[to, 0], tbuf[to, 1]], axis=1), w, 0)
            for k in range(2):
                send[:, to, k] = both[:, k * HIGH : (k + 1) * HIGH].T.reshape(TILES, 8, HIGH)
        return c

    with jax.named_scope("A2"):
        lax.fori_loop(0, 8, width_last, 0)
    mask_copy = pltpu.make_async_remote_copy(
        mask_ref, mask_in, par_send.at[0], par_recv.at[0], device_id=(other, row), device_id_type=MESH
    )
    level_copy = pltpu.make_async_remote_copy(
        level_out, level_in, par_send.at[1], par_recv.at[1], device_id=(other, row), device_id_type=MESH
    )
    mask_copy.start()
    level_copy.start()
    lax.fori_loop(28, 32, lambda i, c: (exchange(0, 0, 2, peer(i)).start(), c)[1], 0)
    exchange_all(1, 2, 2)

    mask_copy.wait()
    level_copy.wait()
    distance = 100.0 + 2.0 * level_in[...]

    def cutoff(k):
        total = jnp.sum(mask_in[0, k : k + 1, :].astype(F32), axis=1, keepdims=True)
        return jnp.broadcast_to((total + 1.0) * 0.5, (8, HIGH))[None]

    cut_y, cut_x = cutoff(0), cutoff(1)
    shape = (8, 8, HIGH)

    def signed(k):
        return jnp.where(k < N // 2, k, k - N).astype(F32)

    def propagate(i, c):
        t, g = i // 4, lax.rem(i, 4)
        k_y = signed(lax.broadcasted_iota(jnp.int32, shape, 0) + g * 8 + 32 * lax.broadcasted_iota(jnp.int32, shape, 2))
        k_x = signed(row + 32 * (t * 8 + lax.broadcasted_iota(jnp.int32, shape, 1)))
        f_y, f_x = k_y * (1.0 / N), k_x * (1.0 / N)
        square = f_y * f_y + f_x * f_x
        quarters = (-4.0 * distance[None]) * (square / (2.0 + jnp.sqrt(4.0 - square)))
        whole = jnp.floor(quarters + 0.5)
        v = (quarters - whole) * (0.5 * math.pi)
        quadrant = whole - 4.0 * jnp.floor(whole * 0.25)
        v2 = v * v
        sine = v + v * v2 * (-1.6666654611e-1 + v2 * (8.3321608736e-3 - v2 * 1.9515295891e-4))
        cosine = 1.0 - 0.5 * v2 + v2 * v2 * (4.166664568298827e-2 + v2 * (-1.388731625493765e-3 + v2 * 2.443315711809948e-5))
        odd = (quadrant == 1.0) | (quadrant == 3.0)
        re = jnp.where(odd, sine, cosine)
        im = jnp.where(odd, cosine, sine)
        inside = (jnp.abs(k_y) < cut_y) & (jnp.abs(k_x) < cut_x)
        weight = jnp.where(inside, 1.0, 0.0)
        prop[t, pl.ds(g * 8, 8), 0] = jnp.where((quadrant == 1.0) | (quadrant == 2.0), -re, re) * weight
        prop[t, pl.ds(g * 8, 8), 1] = jnp.where(quadrant >= 2.0, -im, im) * weight
        return c

    with jax.named_scope("H"):
        lax.fori_loop(0, 4 * TILES, propagate, 0)

    def height(t, c):
        re, im = joined(dft32(recv[t, :, 0], recv[t, :, 1], small, -1))
        cosine, sine = turn[0], turn[1]
        re, im = along_lanes(re * cosine + im * sine, im * cosine - re * sine, w, 0)
        p_re, p_im = prop[t, :, 0], prop[t, :, 1]
        re, im = along_lanes(re * p_re - im * p_im, re * p_im + im * p_re, w, 2)
        re, im = joined(dft32(re * cosine - im * sine, im * cosine + re * sine, small, 1))
        part[t, :, 0] = re
        part[t, :, 1] = im
        return c

    def ring_copy(q, t0, n, step, source):
        tiles = pl.ds(t0, n)
        return pltpu.make_async_remote_copy(
            part.at[tiles, pl.ds(source * 4, 4)], ring.at[tiles, step], ring_send.at[q, step], ring_recv.at[q, step],
            device_id=(up if step < 4 else down, row), device_id_type=MESH,
        )

    def ring_step(q, t0, n, step):
        tiles = pl.ds(t0, n)
        lines = [(step, lax.rem(z + 4 - step, Z))] + ([(step + 4, lax.rem(z + 5 + step, Z))] if step < 3 else [])
        for i, source in lines:
            if step > 0:
                ring_copy(q, t0, n, i - 1, source).wait_recv()
                block = pl.ds(source * 4, 4)
                part[tiles, block] = part[tiles, block] + ring[tiles, i - 1]
        for i, source in lines:
            ring_copy(q, t0, n, i, source).start()

    def pair_copy(q, t0, n):
        tiles = pl.ds(t0, n)
        return pltpu.make_async_remote_copy(
            own.at[tiles, pl.ds(y_lo * 2, 2)], pair.at[tiles], pair_send.at[q], pair_recv.at[q],
            device_id=(other, row), device_id_type=MESH,
        )

    def ring_end(q, t0, n):
        tiles = pl.ds(t0, n)
        ring_copy(q, t0, n, 6, z).wait_recv()
        ring_copy(q, t0, n, 3, z).wait_recv()
        own[tiles] = part[tiles, pl.ds(z * 4, 4)] + (ring[tiles, 3] + ring[tiles, 6])
        pair_copy(q, t0, n).start()

    def chunk(q, t0, n, before, ahead, between=None):
        with jax.named_scope("wait_a2a"):
            exchange_whole(q, t0, n).wait_recv()
        with jax.named_scope("C"):
            lax.fori_loop(t0, t0 + n, height, 0)
        ring_step(q, t0, n, 0)
        ahead()
        with jax.named_scope("ring"):
            if before is not None:
                ring_step(*before, 3)
            ring_step(q, t0, n, 1)
            if between is not None:
                between()
            if before is not None:
                ring_end(*before)
            ring_step(q, t0, n, 2)

    keep = 2 - 2 * y_lo

    def deliver(half, to):
        return pltpu.make_async_remote_copy(
            final.at[half, to], final_in.at[half, row], final_send.at[half], final_recv.at[half],
            device_id=(other, to), device_id_type=MESH,
        )

    def deliver_whole(half):
        return pltpu.make_async_remote_copy(
            final.at[half], final_in.at[half], final_send.at[half], final_recv.at[half],
            device_id=(other, row), device_id_type=MESH,
        )

    def hand_over(half):
        tiles = pl.ds(half * 8, 8)
        for a in range(2):
            block = [(own[tiles, keep + a, k] + pair[tiles, a, k]).reshape(64, HIGH) for k in range(2)]
            final[half, a * 16 : a * 16 + 16] = jnp.concatenate(block).T.reshape(16, 8, HIGH)

        def some(i, c):
            for h in range(4):
                deliver(half, peer(i * 4 + h)).start()
            return c

        lax.fori_loop(0, 8, some, 0)

    def first_half():
        for q in range(4):
            pair_copy(q, 2 * q, 2).wait_recv()
        hand_over(0)

    chunk(0, 0, 2, None, lambda: exchange_all(2, 4, 2))

    def middle(q, c):
        def ahead():
            @pl.when(q < WIDE - 2)
            def _():
                exchange_all(q + 2, 2 * q + 4, 2)

            @pl.when(q >= WIDE - 2)
            def _():
                exchange_all(q + 2, q + 2 + WIDE, 1)

        chunk(q, 2 * q, 2, (q - 1, 2 * q - 2, 2), ahead)
        return c

    lax.fori_loop(1, WIDE, middle, 0)
    chunk(WIDE, 14, 1, (WIDE - 1, 12, 2), lambda: None)
    chunk(WIDE + 1, 15, 1, (WIDE, 14, 1), lambda: None, first_half)
    with jax.named_scope("last_ring"):
        ring_step(WIDE + 1, 15, 1, 3)
        ring_end(WIDE + 1, 15, 1)
    with jax.named_scope("pair_wait"):
        for q in range(4, WIDE):
            pair_copy(q, 2 * q, 2).wait_recv()
        for q in range(WIDE, CHUNKS):
            pair_copy(q, q + WIDE, 1).wait_recv()
    hand_over(1)

    def settle(q, t0, n):
        exchange_whole(q, t0, n).wait_send()
        pair_copy(q, t0, n).wait_send()
        for step in range(7):
            ring_copy(q, t0, n, step, z).wait_send()

    lax.fori_loop(0, WIDE, lambda q, c: (settle(q, 2 * q, 2), c)[1], 0)
    for q in range(WIDE, CHUNKS):
        settle(q, q + WIDE, 1)
    with jax.named_scope("final_wait"):
        deliver_whole(0).wait_recv()
        deliver_whole(1).wait_recv()

    left = jnp.concatenate([final_in[0].reshape(8 * LOW, HIGH), final_in[1].reshape(8 * LOW, HIGH)], axis=1)
    both = split_dot(left, w, 4)
    re, im = both[:, :HIGH].reshape(LOW, 8, HIGH), both[:, HIGH:].reshape(LOW, 8, HIGH)
    cosine, sine = turn[0] * 0.25, turn[1] * 0.25
    pieces = dft32(re * cosine - im * sine, im * cosine + re * sine, small, 1)
    for k in range(8):
        for j in range(4):
            lanes = pl.ds((k * 4 + j) * HIGH, HIGH)
            out_ref[0, :, lanes] = pieces[k][0][j]
            out_ref[1, :, lanes] = pieces[k][1][j]
    deliver_whole(0).wait_send()
    deliver_whole(1).wait_send()


def local(target, depth_index, band_mask):
    turn, small, matrices = tables()
    anywhere = pl.BlockSpec(memory_space=pl.ANY)
    dma = pltpu.SemaphoreType.DMA
    return pl.pallas_call(
        kernel,
        out_shape=jax.ShapeDtypeStruct((2, 8, N), F32),
        in_specs=[anywhere] * 6,
        out_specs=pl.BlockSpec(memory_space=pltpu.VMEM),
        scratch_shapes=[
            pltpu.VMEM((2, HIGH, N), F32),
            pltpu.VMEM((LOW, 2, HIGH, HIGH), F32),
            pltpu.VMEM((TILES, LOW, 2, 8, HIGH), F32),
            pltpu.VMEM((TILES, LOW, 2, 8, HIGH), F32),
            pltpu.VMEM((TILES, LOW, 2, 8, HIGH), F32),
            pltpu.VMEM((TILES, LOW, 2, 8, HIGH), F32),
            pltpu.VMEM((TILES, 7, 4, 2, 8, HIGH), F32),
            pltpu.VMEM((TILES, 4, 2, 8, HIGH), F32),
            pltpu.VMEM((TILES, 2, 2, 8, HIGH), F32),
            pltpu.VMEM((2, LOW, 8, HIGH), F32),
            pltpu.VMEM((2, LOW, 8, HIGH), F32),
            pltpu.VMEM((1, 2, N), jnp.int32),
            pltpu.SMEM((1,), jnp.int32),
            pltpu.VMEM((8, HIGH), F32),
            pltpu.VMEM((8, HIGH), F32),
            pltpu.VMEM(turn.shape, F32),
            pltpu.VMEM(small.shape, F32),
            pltpu.VMEM(matrices.shape, BF16),
            dma((4,)),
            dma((4,)),
            dma((CHUNKS,)),
            dma((CHUNKS,)),
            dma((CHUNKS, 7)),
            dma((CHUNKS, 7)),
            dma((CHUNKS,)),
            dma((CHUNKS,)),
            dma((2,)),
            dma((2,)),
            dma((2,)),
            dma((2,)),
        ],
        compiler_params=pltpu.CompilerParams(
            collective_id=0, has_side_effects=True, vmem_limit_bytes=60 * 1024 * 1024
        ),
        name="hologram",
    )(target, band_mask, depth_index, turn, small, matrices)


def solution(mesh):
    in_specs = (P("depth", None, "rows", None), P("depth"), P("depth", None, None))
    out_specs = P(None, ("depth", "rows"), None)
    return jax.shard_map(local, mesh=mesh, in_specs=in_specs, out_specs=out_specs, check_vma=False)
```

time: 155 us -> 148 us (0.955)
  Pallas kernels: 150 us -> 145 us
  local copies, waits for them, and re-layouts: 3.64 us -> 1.67 us
    pallas_call x1, Pallas kernels: 150 us -> 145 us  [local(): pl.pallas_call(kernel, out_shape=jax.ShapeDtypeStruct((2, 8, N), F32), in...]
where the time goes in v1:
time: 148 us
  Pallas kernels  145 us (98%)
  local copies, waits for them, and re-layouts  1.67 us (1%)
    pallas_call x1, Pallas kernels, local(): pl.pallas_call(kernel, out_shape=jax.ShapeDtypeStruct((2, 8, N), F32), in...  145 us

profile of v1, /device:TPU:1, one launch (start us, length us, event | category | flops | bytes accessed | tf_op | source)
XLA Modules:
  0.0 147.6 jit_solution(171991444479137226)
XLA Ops:
  0.7 145.3 %hologram.1 = f32[2,8,4096]{2,1,0:T(8,128)} custom-call(f32[1,2,128,4096]{3,2,1,0:T(8,128)} %x_ref.1, s32[1,2,4096]{2,1,0:T(2,128)} %mask_ref.1, s32[1]{0:T(128)S(6)} %copy.8.level_ref, f32[2,32,8,128]{3,2,1,0:T(8,128)} %constant.6.clone.turn_ref, f32[2,3,8,8,128]{4,3,2,1,0:T(8,128)} %constant.7.clone.small_ref, bf16[6,256,256]{2,1,0:T(8,128)(2,1)} %constant.8.clone.w_ref), custom_call_target="tpu_custom_call" | custom-call | tf_op jit(solution)/shard_map/hologram/pallas_call | solution.py:404
  146.0 1.7 %copy.9 = f32[2,8,4096]{2,1,0:T(8,128)} copy(f32[2,8,4096]{2,1,0:T(8,128)} %hologram.1) | data formatting | bytes 524288

commit v2 on v1

--- a/solution.py
+++ b/solution.py
@@ -18,6 +18,8 @@
 TILES = 16
 WIDE = 7
 CHUNKS = WIDE + 2
+LAST = TILES - 1
+FAR = (4, 3, 5, 2, 6, 1, 7)
 F32 = jnp.float32
 BF16 = jnp.bfloat16
 
@@ -39,7 +41,13 @@
         parts += [top, rest]
     order = np.arange(256).reshape(2, 2, 64).swapaxes(0, 1).reshape(256)
     parts += [parts[2][order], parts[3][order]]
-    return turn, small, np.stack(parts)
+    angle = 2.0 * np.pi / LOW * np.outer(np.arange(LOW), np.arange(LOW))
+    cosine, sine = np.cos(angle), np.sin(angle)
+    short = np.block([[cosine, -sine], [sine, cosine]])
+    short = short.reshape(2, Z, 4, 2 * LOW).swapaxes(0, 1).reshape(2 * LOW, 2 * LOW)
+    top = short.astype(np.float32).astype(ml_dtypes.bfloat16)
+    rest = (short - top.astype(np.float64)).astype(np.float32).astype(ml_dtypes.bfloat16)
+    return turn, small, np.stack(parts), turn[:, :, 0, :].copy(), np.stack([top, rest])
 
 
 def dft4(a, sign):
@@ -92,11 +100,11 @@
 
 
 def kernel(
-    x_ref, mask_ref, level_ref, turn_ref, small_ref, w_ref, out_ref,
+    x_ref, mask_ref, level_ref, turn_ref, small_ref, w_ref, flat_ref, short_ref, out_ref,
     xbuf, tbuf, send, recv, prop, part, ring, own, pair, final, final_in, mask_in, level_at, level_out, level_in,
-    turn, small, w,
+    turn, small, w, flat, short, z_out, z_in, par_out, par_in, sum_out, sum_in,
     x_sem, in_sem, send_sem, recv_sem, ring_send, ring_recv, pair_send, pair_recv, final_send, final_recv,
-    par_send, par_recv,
+    par_send, par_recv, z_send, z_recv, all_send, all_recv, sum_send, sum_recv,
 ):
     depth = lax.axis_index("depth")
     row = lax.axis_index("rows")
@@ -111,6 +119,12 @@
         to_core = lax.rem(core + lax.rem(i // 4, 2), 2)
         to_x = lax.rem(x + i // 8, 4)
         return (to_x * 4 + to_y) * 2 + to_core
+
+    xs = [lax.rem(x + k, 4) for k in range(4)]
+    ys = [lax.rem(y_hi + y_lo + k, 4) for k in range(4)]
+    cores = [core, 1 - core]
+    near_first = [(xs[i] * 4 + ys[h]) * 2 + c for i in range(4) for c in cores for h in (1, 2, 0, 3)]
+    far_first = [(xs[i] * 4 + ys[h]) * 2 + c for i in (2, 1, 3, 0) for h in (1, 2, 0, 3) for c in cores]
 
     def load(g):
         rows = pl.ds(pl.multiple_of(g * 32, 32), 32)
@@ -127,6 +141,10 @@
         load(g).start()
     load_w.start()
     load_level.start()
+    load_flat = pltpu.make_async_copy(flat_ref, flat, in_sem.at[4])
+    load_short = pltpu.make_async_copy(short_ref, short, in_sem.at[5])
+    load_flat.start()
+    load_short.start()
 
     barrier = pltpu.get_barrier_semaphore()
 
@@ -135,8 +153,8 @@
         return c
 
     lax.fori_loop(0, 32, greet, 0)
-    pl.semaphore_signal(barrier, inc=1, device_id=(up, row), device_id_type=MESH)
-    pl.semaphore_signal(barrier, inc=1, device_id=(down, row), device_id_type=MESH)
+    for k in FAR:
+        pl.semaphore_signal(barrier, inc=1, device_id=(2 * lax.rem(z + k, Z) + y_lo, row), device_id_type=MESH)
 
     load_small.wait()
     load_turn.wait()
@@ -160,8 +178,10 @@
     load_level.wait()
     level_out[...] = jnp.full((8, HIGH), level_at[0].astype(F32))
     load_w.wait()
+    load_flat.wait()
+    load_short.wait()
     with jax.named_scope("barrier"):
-        pl.semaphore_wait(barrier, 34)
+        pl.semaphore_wait(barrier, 39)
 
     def exchange(q, t0, n, to):
         tiles = pl.ds(t0, n)
@@ -178,12 +198,22 @@
         )
 
     def exchange_all(q, t0, n):
-        def some(i, c):
-            for h in range(4):
-                exchange(q, t0, n, peer(i * 4 + h)).start()
-            return c
-
-        lax.fori_loop(0, 8, some, 0)
+        for to in near_first:
+            exchange(q, t0, n, to).start()
+
+    def along_z(out, into, send_sems, recv_sems, k, shared=False):
+        to = lax.rem(z + k, Z)
+        return pltpu.make_async_remote_copy(
+            out if shared else out.at[to], into.at[z], send_sems.at[k], recv_sems.at[z],
+            device_id=(2 * to + y_lo, row), device_id_type=MESH,
+        )
+
+    def from_z(out, into, send_sems, recv_sems, k, shared=False):
+        source = lax.rem(z + k, Z)
+        return pltpu.make_async_remote_copy(
+            out if shared else out.at[source], into.at[source], send_sems.at[k], recv_sems.at[source],
+            device_id=(2 * source + y_lo, row), device_id_type=MESH,
+        )
 
     def width_last(g, c):
         @pl.when(g > 0)
@@ -200,6 +230,9 @@
 
     with jax.named_scope("A2"):
         lax.fori_loop(0, 8, width_last, 0)
+    for g in range(8):
+        block = send[LAST, 4 * g : 4 * g + 4].reshape(8, 8, HIGH)
+        z_out[:, 8 * g : 8 * g + 8, :] = jnp.swapaxes(block, 0, 1)
     mask_copy = pltpu.make_async_remote_copy(
         mask_ref, mask_in, par_send.at[0], par_recv.at[0], device_id=(other, row), device_id_type=MESH
     )
@@ -209,6 +242,9 @@
     mask_copy.start()
     level_copy.start()
     lax.fori_loop(28, 32, lambda i, c: (exchange(0, 0, 2, peer(i)).start(), c)[1], 0)
+    for k in FAR:
+        along_z(z_out, z_in, z_send, z_recv, k).start()
+    z_in[z] = z_out[z]
     exchange_all(1, 2, 2)
 
     mask_copy.wait()
@@ -217,18 +253,20 @@
 
     def cutoff(k):
         total = jnp.sum(mask_in[0, k : k + 1, :].astype(F32), axis=1, keepdims=True)
-        return jnp.broadcast_to((total + 1.0) * 0.5, (8, HIGH))[None]
+        return jnp.broadcast_to((total + 1.0) * 0.5, (8, HIGH))
 
     cut_y, cut_x = cutoff(0), cutoff(1)
+    line = lax.broadcasted_iota(jnp.int32, (8, HIGH), 0)
+    about = jnp.where(line == 0, distance, jnp.where(line == 1, cut_y, cut_x))
+    par_out[...] = about
+    par_in[z] = about
     shape = (8, 8, HIGH)
 
     def signed(k):
         return jnp.where(k < N // 2, k, k - N).astype(F32)
 
-    def propagate(i, c):
-        t, g = i // 4, lax.rem(i, 4)
+    def propagate(t, g, k_x, distance, cut_y, cut_x):
         k_y = signed(lax.broadcasted_iota(jnp.int32, shape, 0) + g * 8 + 32 * lax.broadcasted_iota(jnp.int32, shape, 2))
-        k_x = signed(row + 32 * (t * 8 + lax.broadcasted_iota(jnp.int32, shape, 1)))
         f_y, f_x = k_y * (1.0 / N), k_x * (1.0 / N)
         square = f_y * f_y + f_x * f_x
         quarters = (-4.0 * distance[None]) * (square / (2.0 + jnp.sqrt(4.0 - square)))
@@ -241,14 +279,36 @@
         odd = (quadrant == 1.0) | (quadrant == 3.0)
         re = jnp.where(odd, sine, cosine)
         im = jnp.where(odd, cosine, sine)
-        inside = (jnp.abs(k_y) < cut_y) & (jnp.abs(k_x) < cut_x)
+        inside = (jnp.abs(k_y) < cut_y[None]) & (jnp.abs(k_x) < cut_x[None])
         weight = jnp.where(inside, 1.0, 0.0)
         prop[t, pl.ds(g * 8, 8), 0] = jnp.where((quadrant == 1.0) | (quadrant == 2.0), -re, re) * weight
         prop[t, pl.ds(g * 8, 8), 1] = jnp.where(quadrant >= 2.0, -im, im) * weight
+
+    def propagate_tile(i, c):
+        t, g = i // 4, lax.rem(i, 4)
+        k_x = signed(row + 32 * (t * 8 + lax.broadcasted_iota(jnp.int32, shape, 1)))
+        propagate(t, g, k_x, distance, cut_y, cut_x)
         return c
 
     with jax.named_scope("H"):
-        lax.fori_loop(0, 4 * TILES, propagate, 0)
+        lax.fori_loop(0, 4 * LAST, propagate_tile, 0)
+    for k in FAR:
+        along_z(par_out, par_in, all_send, all_recv, k, True).start()
+
+    def prepare_last():
+        for k in FAR:
+            from_z(z_out, z_in, z_send, z_recv, k).wait_recv()
+            from_z(par_out, par_in, all_send, all_recv, k, True).wait_recv()
+        for g in range(8):
+            send[LAST, 4 * g : 4 * g + 4] = jnp.swapaxes(z_in[:, 8 * g : 8 * g + 8, :], 0, 1).reshape(4, 2, 8, HIGH)
+        each = [jnp.concatenate([par_in[p, j : j + 1, :] for p in range(8)]) for j in range(3)]
+        k_x = signed(jnp.full(shape, row + 32 * (8 * LAST + z), jnp.int32))
+
+        def group(g, c):
+            propagate(LAST, g, k_x, *each)
+            return c
+
+        lax.fori_loop(0, 4, group, 0)
 
     def height(t, c):
         re, im = joined(dft32(recv[t, :, 0], recv[t, :, 1], small, -1))
@@ -261,6 +321,25 @@
         part[t, :, 1] = im
         return c
 
+    def height_last():
+        re, im = joined(dft32(recv[LAST, :, 0], recv[LAST, :, 1], small, -1))
+        cosine, sine = turn[0], turn[1]
+        re, im = along_lanes(re * cosine + im * sine, im * cosine - re * sine, w, 0)
+        p_re, p_im = prop[LAST, :, 0], prop[LAST, :, 1]
+        left = jnp.concatenate(
+            [jnp.sum(re * p_re - im * p_im, axis=1), jnp.sum(re * p_im + im * p_re, axis=1)], axis=1
+        )
+        both = split_dot(left, w, 2)
+        re, im = both[:, :HIGH], both[:, HIGH:]
+        cosine, sine = flat[0], flat[1]
+        right = jnp.concatenate([re * cosine - im * sine, im * cosine + re * sine])
+        top = right.astype(BF16)
+        rest = (right - top.astype(F32)).astype(BF16)
+        dot = functools.partial(jnp.dot, preferred_element_type=F32)
+        result = dot(short[0], top) + (dot(short[0], rest) + dot(short[1], top))
+        sum_out[...] = result.reshape(Z, 8, HIGH)
+        sum_in[z] = sum_out[z]
+
     def ring_copy(q, t0, n, step, source):
         tiles = pl.ds(t0, n)
         return pltpu.make_async_remote_copy(
@@ -293,7 +372,7 @@
         own[tiles] = part[tiles, pl.ds(z * 4, 4)] + (ring[tiles, 3] + ring[tiles, 6])
         pair_copy(q, t0, n).start()
 
-    def chunk(q, t0, n, before, ahead, between=None):
+    def chunk(q, t0, n, before, ahead):
         with jax.named_scope("wait_a2a"):
             exchange_whole(q, t0, n).wait_recv()
         with jax.named_scope("C"):
@@ -304,11 +383,10 @@
             if before is not None:
                 ring_step(*before, 3)
             ring_step(q, t0, n, 1)
-            if between is not None:
-                between()
             if before is not None:
                 ring_end(*before)
-            ring_step(q, t0, n, 2)
+            if q is not WIDE:
+                ring_step(q, t0, n, 2)
 
     keep = 2 - 2 * y_lo
 
@@ -330,55 +408,75 @@
             block = [(own[tiles, keep + a, k] + pair[tiles, a, k]).reshape(64, HIGH) for k in range(2)]
             final[half, a * 16 : a * 16 + 16] = jnp.concatenate(block).T.reshape(16, 8, HIGH)
 
-        def some(i, c):
-            for h in range(4):
-                deliver(half, peer(i * 4 + h)).start()
-            return c
-
-        lax.fori_loop(0, 8, some, 0)
-
-    def first_half():
+    def dispatch(half):
+        for to in far_first:
+            deliver(half, to).start()
+
+    chunk(0, 0, 2, None, lambda: exchange_all(2, 4, 2))
+
+    def middle(q, c):
+        def ahead():
+            @pl.when(q == 3)
+            def _():
+                prepare_last()
+
+            @pl.when(q < WIDE - 2)
+            def _():
+                exchange_all(q + 2, 2 * q + 4, 2)
+
+            @pl.when(q >= WIDE - 2)
+            def _():
+                exchange_all(q + 2, q + 2 + WIDE, 1)
+
+        chunk(q, 2 * q, 2, (q - 1, 2 * q - 2, 2), ahead)
+        return c
+
+    lax.fori_loop(1, WIDE, middle, 0)
+    chunk(WIDE, 14, 1, (WIDE - 1, 12, 2), lambda: None)
+    with jax.named_scope("first_half"):
         for q in range(4):
             pair_copy(q, 2 * q, 2).wait_recv()
         hand_over(0)
-
-    chunk(0, 0, 2, None, lambda: exchange_all(2, 4, 2))
-
-    def middle(q, c):
-        def ahead():
-            @pl.when(q < WIDE - 2)
-            def _():
-                exchange_all(q + 2, 2 * q + 4, 2)
-
-            @pl.when(q >= WIDE - 2)
-            def _():
-                exchange_all(q + 2, q + 2 + WIDE, 1)
-
-        chunk(q, 2 * q, 2, (q - 1, 2 * q - 2, 2), ahead)
-        return c
-
-    lax.fori_loop(1, WIDE, middle, 0)
-    chunk(WIDE, 14, 1, (WIDE - 1, 12, 2), lambda: None)
-    chunk(WIDE + 1, 15, 1, (WIDE, 14, 1), lambda: None, first_half)
+    with jax.named_scope("wait_last"):
+        exchange_whole(WIDE + 1, LAST, 1).wait_recv()
+    with jax.named_scope("C_last"):
+        height_last()
+    for k in FAR:
+        along_z(sum_out, sum_in, sum_send, sum_recv, k).start()
     with jax.named_scope("last_ring"):
-        ring_step(WIDE + 1, 15, 1, 3)
-        ring_end(WIDE + 1, 15, 1)
+        ring_step(WIDE, 14, 1, 2)
+        dispatch(0)
+        ring_step(WIDE, 14, 1, 3)
+    with jax.named_scope("last_sum"):
+        for k in FAR:
+            from_z(sum_out, sum_in, sum_send, sum_recv, k).wait_recv()
+        lines = jnp.swapaxes(sum_in[...], 0, 1)
+        for k in range(2):
+            own[LAST, :, k] = lines[4 * k : 4 * k + 4]
+        pair_copy(WIDE + 1, LAST, 1).start()
+        ring_end(WIDE, 14, 1)
     with jax.named_scope("pair_wait"):
         for q in range(4, WIDE):
             pair_copy(q, 2 * q, 2).wait_recv()
         for q in range(WIDE, CHUNKS):
             pair_copy(q, q + WIDE, 1).wait_recv()
     hand_over(1)
+    dispatch(1)
 
     def settle(q, t0, n):
         exchange_whole(q, t0, n).wait_send()
         pair_copy(q, t0, n).wait_send()
-        for step in range(7):
-            ring_copy(q, t0, n, step, z).wait_send()
+        if t0 is not LAST:
+            for step in range(7):
+                ring_copy(q, t0, n, step, z).wait_send()
 
     lax.fori_loop(0, WIDE, lambda q, c: (settle(q, 2 * q, 2), c)[1], 0)
-    for q in range(WIDE, CHUNKS):
-        settle(q, q + WIDE, 1)
+    settle(WIDE, LAST - 1, 1)
+    settle(WIDE + 1, LAST, 1)
+    for k in FAR:
+        along_z(z_out, z_in, z_send, z_recv, k).wait_send()
+        along_z(par_out, par_in, all_send, all_recv, k, True).wait_send()
+        along_z(sum_out, sum_in, sum_send, sum_recv, k).wait_send()
     with jax.named_scope("final_wait"):
         deliver_whole(0).wait_recv()
         deliver_whole(1).wait_recv()
@@ -398,13 +496,13 @@
 
 
 def local(target, depth_index, band_mask):
-    turn, small, matrices = tables()
+    turn, small, matrices, flat, short = tables()
     anywhere = pl.BlockSpec(memory_space=pl.ANY)
     dma = pltpu.SemaphoreType.DMA
     return pl.pallas_call(
         kernel,
         out_shape=jax.ShapeDtypeStruct((2, 8, N), F32),
-        in_specs=[anywhere] * 6,
+        in_specs=[anywhere] * 8,
         out_specs=pl.BlockSpec(memory_space=pltpu.VMEM),
         scratch_shapes=[
             pltpu.VMEM((2, HIGH, N), F32),
@@ -425,8 +523,16 @@
             pltpu.VMEM(turn.shape, F32),
             pltpu.VMEM(small.shape, F32),
             pltpu.VMEM(matrices.shape, BF16),
+            pltpu.VMEM(flat.shape, F32),
+            pltpu.VMEM(short.shape, BF16),
+            pltpu.VMEM((Z, 2 * LOW, HIGH), F32),
+            pltpu.VMEM((Z, 2 * LOW, HIGH), F32),
+            pltpu.VMEM((8, HIGH), F32),
+            pltpu.VMEM((Z, 8, HIGH), F32),
+            pltpu.VMEM((Z, 8, HIGH), F32),
+            pltpu.VMEM((Z, 8, HIGH), F32),
             dma((4,)),
-            dma((4,)),
+            dma((6,)),
             dma((CHUNKS,)),
             dma((CHUNKS,)),
             dma((CHUNKS, 7)),
@@ -437,12 +543,18 @@
             dma((2,)),
             dma((2,)),
             dma((2,)),
+            dma((Z,)),
+            dma((Z,)),
+            dma((Z,)),
+            dma((Z,)),
+            dma((Z,)),
+            dma((Z,)),
         ],
         compiler_params=pltpu.CompilerParams(
             collective_id=0, has_side_effects=True, vmem_limit_bytes=60 * 1024 * 1024
         ),
         name="hologram",
-    )(target, band_mask, depth_index, turn, small, matrices)
+    )(target, band_mask, depth_index, turn, small, matrices, flat, short)
 
 
 def solution(mesh):

time: 148 us -> 140 us (0.946)
  Pallas kernels: 145 us -> 137 us
    pallas_call x1, Pallas kernels: 145 us -> 137 us  [local(): pl.pallas_call(kernel, out_shape=jax.ShapeDtypeStruct((2, 8, N), F32), in...]
where the time goes in v2:
time: 140 us
  Pallas kernels  137 us (98%)
  local copies, waits for them, and re-layouts  1.67 us (1%)
    pallas_call x1, Pallas kernels, local(): pl.pallas_call(kernel, out_shape=jax.ShapeDtypeStruct((2, 8, N), F32), in...  137 us

profile of v2, /device:TPU:1, one launch (start us, length us, event | category | flops | bytes accessed | tf_op | source)
XLA Modules:
  0.0 139.6 jit_solution(10895005303382768654)
XLA Ops:
  0.7 137.3 %hologram.1 = f32[2,8,4096]{2,1,0:T(8,128)} custom-call(f32[1,2,128,4096]{3,2,1,0:T(8,128)} %x_ref.1, s32[1,2,4096]{2,1,0:T(2,128)} %mask_ref.1, s32[1]{0:T(128)S(6)} %copy.10.level_ref, f32[2,32,8,128]{3,2,1,0:T(8,128)} %constant.10.clone.turn_ref, f32[2,3,8,8,128]{4,3,2,1,0:T(8,128)} %constant.11.clone.small_ref, ...), custom_call_target="tpu_custom_call" | custom-call | tf_op jit(solution)/shard_map/hologram/pallas_call | solution.py:502
  138.0 1.7 %copy.11 = f32[2,8,4096]{2,1,0:T(8,128)} copy(f32[2,8,4096]{2,1,0:T(8,128)} %hologram.1) | data formatting | bytes 524288

commit v3 on v2

--- a/solution.py
+++ b/solution.py
@@ -16,9 +16,11 @@
 HIGH = 128
 Z = 8
 TILES = 16
-WIDE = 7
-CHUNKS = WIDE + 2
-LAST = TILES - 1
+WIDE = 6
+SINGLE = 4
+CHUNKS = WIDE + SINGLE
+ALONE = 2 * WIDE
+PAIRED = (0, 8, 15, 16)
 FAR = (4, 3, 5, 2, 6, 1, 7)
 F32 = jnp.float32
 BF16 = jnp.bfloat16
@@ -85,10 +87,10 @@
     return jnp.concatenate([p[0] for p in pieces]), jnp.concatenate([p[1] for p in pieces])
 
 
-def split_dot(left, w_ref, which):
+def split_dot(left, w_ref, which, rows=slice(None)):
     top = left.astype(BF16)
     rest = (left - top.astype(F32)).astype(BF16)
-    w_top, w_rest = w_ref[which], w_ref[which + 1]
+    w_top, w_rest = w_ref[which, rows], w_ref[which + 1, rows]
     dot = functools.partial(jnp.dot, preferred_element_type=F32)
     return dot(top, w_top) + (dot(rest, w_top) + dot(top, w_rest))
 
@@ -113,18 +115,24 @@
     other = depth + 1 - 2 * y_lo
     up, down = lax.rem(depth + 2, 2 * Z), lax.rem(depth + 2 * Z - 2, 2 * Z)
 
+    column = (x * 4 + lax.rem(y_hi + y_lo * core, 4)) * 2 + core
+    mate = (x * 4 + lax.rem(y_hi + core * (3 - 2 * y_lo), 4)) * 2 + core
+
+    def place(to_x, to_y, to_core):
+        return (to_x * 4 + to_y) * 2 + to_core, (to_x * 4 + lax.rem(to_y + to_core * (1 - y_lo), 4)) * 2 + to_core
+
     def peer(i):
         h = lax.rem(i, 4)
         to_y = lax.rem(y_hi + lax.rem(h, 2) * 2 + h // 2, 4)
         to_core = lax.rem(core + lax.rem(i // 4, 2), 2)
         to_x = lax.rem(x + i // 8, 4)
-        return (to_x * 4 + to_y) * 2 + to_core
+        return place(to_x, to_y, to_core)
 
     xs = [lax.rem(x + k, 4) for k in range(4)]
     ys = [lax.rem(y_hi + y_lo + k, 4) for k in range(4)]
     cores = [core, 1 - core]
-    near_first = [(xs[i] * 4 + ys[h]) * 2 + c for i in range(4) for c in cores for h in (1, 2, 0, 3)]
-    far_first = [(xs[i] * 4 + ys[h]) * 2 + c for i in (2, 1, 3, 0) for h in (1, 2, 0, 3) for c in cores]
+    near_first = [place(xs[i], ys[h], c) for i in range(4) for c in cores for h in (1, 2, 0, 3)]
+    far_first = [place(xs[i], ys[h], c) for i in (2, 1, 3, 0) for h in (1, 2, 0, 3) for c in cores]
 
     def load(g):
         rows = pl.ds(pl.multiple_of(g * 32, 32), 32)
@@ -182,57 +190,6 @@
     load_short.wait()
     with jax.named_scope("barrier"):
         pl.semaphore_wait(barrier, 39)
-
-    def exchange(q, t0, n, to):
-        tiles = pl.ds(t0, n)
-        return pltpu.make_async_remote_copy(
-            send.at[tiles, to], recv.at[tiles, row], send_sem.at[q], recv_sem.at[q],
-            device_id=(other, to), device_id_type=MESH,
-        )
-
-    def exchange_whole(q, t0, n):
-        tiles = pl.ds(t0, n)
-        return pltpu.make_async_remote_copy(
-            send.at[tiles], recv.at[tiles], send_sem.at[q], recv_sem.at[q],
-            device_id=(other, row), device_id_type=MESH,
-        )
-
-    def exchange_all(q, t0, n):
-        for to in near_first:
-            exchange(q, t0, n, to).start()
-
-    def along_z(out, into, send_sems, recv_sems, k, shared=False):
-        to = lax.rem(z + k, Z)
-        return pltpu.make_async_remote_copy(
-            out if shared else out.at[to], into.at[z], send_sems.at[k], recv_sems.at[z],
-            device_id=(2 * to + y_lo, row), device_id_type=MESH,
-        )
-
-    def from_z(out, into, send_sems, recv_sems, k, shared=False):
-        source = lax.rem(z + k, Z)
-        return pltpu.make_async_remote_copy(
-            out if shared else out.at[source], into.at[source], send_sems.at[k], recv_sems.at[source],
-            device_id=(2 * source + y_lo, row), device_id_type=MESH,
-        )
-
-    def width_last(g, c):
-        @pl.when(g > 0)
-        def _():
-            for h in range(4):
-                exchange(0, 0, 2, peer((g - 1) * 4 + h)).start()
-
-        for h in range(4):
-            to = peer(g * 4 + h)
-            both = split_dot(jnp.concatenate([tbuf[to, 0], tbuf[to, 1]], axis=1), w, 0)
-            for k in range(2):
-                send[:, to, k] = both[:, k * HIGH : (k + 1) * HIGH].T.reshape(TILES, 8, HIGH)
-        return c
-
-    with jax.named_scope("A2"):
-        lax.fori_loop(0, 8, width_last, 0)
-    for g in range(8):
-        block = send[LAST, 4 * g : 4 * g + 4].reshape(8, 8, HIGH)
-        z_out[:, 8 * g : 8 * g + 8, :] = jnp.swapaxes(block, 0, 1)
     mask_copy = pltpu.make_async_remote_copy(
         mask_ref, mask_in, par_send.at[0], par_recv.at[0], device_id=(other, row), device_id_type=MESH
     )
@@ -241,10 +198,66 @@
     )
     mask_copy.start()
     level_copy.start()
-    lax.fori_loop(28, 32, lambda i, c: (exchange(0, 0, 2, peer(i)).start(), c)[1], 0)
-    for k in FAR:
-        along_z(z_out, z_in, z_send, z_recv, k).start()
-    z_in[z] = z_out[z]
+
+    def exchange(q, t0, n, to, block):
+        tiles = pl.ds(t0, n)
+        return pltpu.make_async_remote_copy(
+            send.at[tiles, block], recv.at[tiles, row], send_sem.at[q], recv_sem.at[q],
+            device_id=(other, to), device_id_type=MESH,
+        )
+
+    def exchange_whole(q, t0, n):
+        tiles = pl.ds(t0, n)
+        return pltpu.make_async_remote_copy(
+            send.at[tiles], recv.at[tiles], send_sem.at[q], recv_sem.at[q],
+            device_id=(other, row), device_id_type=MESH,
+        )
+
+    def exchange_all(q, t0, n):
+        for to, block in near_first:
+            exchange(q, t0, n, to, block).start()
+
+    def along_z(out, into, send_sems, recv_sems, k, shared=False):
+        to = lax.rem(z + k, Z)
+        return pltpu.make_async_remote_copy(
+            out if shared else out.at[to], into.at[z], send_sems.at[k], recv_sems.at[z],
+            device_id=(2 * to + y_lo, row), device_id_type=MESH,
+        )
+
+    def from_z(out, into, send_sems, recv_sems, k, shared=False):
+        source = lax.rem(z + k, Z)
+        return pltpu.make_async_remote_copy(
+            out if shared else out.at[source], into.at[source], send_sems.at[k], recv_sems.at[source],
+            device_id=(2 * source + y_lo, row), device_id_type=MESH,
+        )
+
+    def width_last(g, c):
+        @pl.when(g > 0)
+        def _():
+            for h in range(4):
+                exchange(0, 0, 2, *peer((g - 1) * 4 + h)).start()
+
+        for h in range(4):
+            _, block = peer(g * 4 + h)
+            both = split_dot(jnp.concatenate([tbuf[block, 0], tbuf[block, 1]], axis=1), w, 0)
+            for k in range(2):
+                send[:, block, k] = both[:, k * HIGH : (k + 1) * HIGH].T.reshape(TILES, 8, HIGH)
+        return c
+
+    with jax.named_scope("A2"):
+        lax.fori_loop(0, 8, width_last, 0)
+    for j in range(SINGLE):
+        for g in range(8):
+            block = send[ALONE + j, 4 * g : 4 * g + 4].reshape(8, 8, HIGH)
+            z_out[j, :, 8 * g : 8 * g + 8, :] = jnp.swapaxes(block, 0, 1)
+    lax.fori_loop(28, 32, lambda i, c: (exchange(0, 0, 2, *peer(i)).start(), c)[1], 0)
+    def apart(j):
+        for k in FAR:
+            along_z(z_out.at[j], z_in.at[j], z_send.at[j], z_recv.at[j], k).start()
+        z_in[j, z] = z_out[j, z]
+
+    apart(0)
+    apart(1)
     exchange_all(1, 2, 2)
 
     mask_copy.wait()
@@ -286,29 +299,33 @@
 
     def propagate_tile(i, c):
         t, g = i // 4, lax.rem(i, 4)
-        k_x = signed(row + 32 * (t * 8 + lax.broadcasted_iota(jnp.int32, shape, 1)))
+        k_x = signed(column + 32 * (t * 8 + lax.broadcasted_iota(jnp.int32, shape, 1)))
         propagate(t, g, k_x, distance, cut_y, cut_x)
         return c
 
     with jax.named_scope("H"):
-        lax.fori_loop(0, 4 * LAST, propagate_tile, 0)
+        lax.fori_loop(0, 4 * ALONE, propagate_tile, 0)
     for k in FAR:
         along_z(par_out, par_in, all_send, all_recv, k, True).start()
 
-    def prepare_last():
+    def prepare_alone():
         for k in FAR:
-            from_z(z_out, z_in, z_send, z_recv, k).wait_recv()
+            for j in range(SINGLE):
+                from_z(z_out.at[j], z_in.at[j], z_send.at[j], z_recv.at[j], k).wait_recv()
             from_z(par_out, par_in, all_send, all_recv, k, True).wait_recv()
-        for g in range(8):
-            send[LAST, 4 * g : 4 * g + 4] = jnp.swapaxes(z_in[:, 8 * g : 8 * g + 8, :], 0, 1).reshape(4, 2, 8, HIGH)
+        for j in range(SINGLE):
+            for g in range(8):
+                block = jnp.swapaxes(z_in[j, :, 8 * g : 8 * g + 8, :], 0, 1)
+                send[ALONE + j, 4 * g : 4 * g + 4] = block.reshape(4, 2, 8, HIGH)
         each = [jnp.concatenate([par_in[p, j : j + 1, :] for p in range(8)]) for j in range(3)]
-        k_x = signed(jnp.full(shape, row + 32 * (8 * LAST + z), jnp.int32))
-
-        def group(g, c):
-            propagate(LAST, g, k_x, *each)
+
+        def group(i, c):
+            t = ALONE + i // 4
+            k_x = signed(jnp.full(shape, column + 32 * (8 * t + z), jnp.int32))
+            propagate(t, lax.rem(i, 4), k_x, *each)
             return c
 
-        lax.fori_loop(0, 4, group, 0)
+        lax.fori_loop(0, 4 * SINGLE, group, 0)
 
     def height(t, c):
         re, im = joined(dft32(recv[t, :, 0], recv[t, :, 1], small, -1))
@@ -321,11 +338,12 @@
         part[t, :, 1] = im
         return c
 
-    def height_last():
-        re, im = joined(dft32(recv[LAST, :, 0], recv[LAST, :, 1], small, -1))
+    def height_alone(j):
+        t = ALONE + j
+        re, im = joined(dft32(recv[t, :, 0], recv[t, :, 1], small, -1))
         cosine, sine = turn[0], turn[1]
         re, im = along_lanes(re * cosine + im * sine, im * cosine - re * sine, w, 0)
-        p_re, p_im = prop[LAST, :, 0], prop[LAST, :, 1]
+        p_re, p_im = prop[t, :, 0], prop[t, :, 1]
         left = jnp.concatenate(
             [jnp.sum(re * p_re - im * p_im, axis=1), jnp.sum(re * p_im + im * p_re, axis=1)], axis=1
         )
@@ -337,8 +355,10 @@
         rest = (right - top.astype(F32)).astype(BF16)
         dot = functools.partial(jnp.dot, preferred_element_type=F32)
         result = dot(short[0], top) + (dot(short[0], rest) + dot(short[1], top))
-        sum_out[...] = result.reshape(Z, 8, HIGH)
-        sum_in[z] = sum_out[z]
+        sum_out[j] = result.reshape(Z, 8, HIGH)
+        sum_in[j, z] = sum_out[j, z]
+        for k in FAR:
+            along_z(sum_out.at[j], sum_in.at[j], sum_send.at[j], sum_recv.at[j], k).start()
 
     def ring_copy(q, t0, n, step, source):
         tiles = pl.ds(t0, n)
@@ -358,11 +378,11 @@
         for i, source in lines:
             ring_copy(q, t0, n, i, source).start()
 
-    def pair_copy(q, t0, n):
-        tiles = pl.ds(t0, n)
+    def pair_copy(q):
+        tiles = pl.ds(PAIRED[q], PAIRED[q + 1] - PAIRED[q])
         return pltpu.make_async_remote_copy(
             own.at[tiles, pl.ds(y_lo * 2, 2)], pair.at[tiles], pair_send.at[q], pair_recv.at[q],
-            device_id=(other, row), device_id_type=MESH,
+            device_id=(other, mate), device_id_type=MESH,
         )
 
     def ring_end(q, t0, n):
@@ -370,29 +390,28 @@
         ring_copy(q, t0, n, 6, z).wait_recv()
         ring_copy(q, t0, n, 3, z).wait_recv()
         own[tiles] = part[tiles, pl.ds(z * 4, 4)] + (ring[tiles, 3] + ring[tiles, 6])
-        pair_copy(q, t0, n).start()
-
-    def chunk(q, t0, n, before, ahead):
+
+    def chunk(q, t0, n, ahead, before=None, ended=None):
         with jax.named_scope("wait_a2a"):
             exchange_whole(q, t0, n).wait_recv()
         with jax.named_scope("C"):
             lax.fori_loop(t0, t0 + n, height, 0)
         ring_step(q, t0, n, 0)
         ahead()
+        if before is not None:
+            ring_step(*before, 2)
+        if ended is not None:
+            ring_end(*ended)
         with jax.named_scope("ring"):
+            ring_step(q, t0, n, 1)
             if before is not None:
                 ring_step(*before, 3)
-            ring_step(q, t0, n, 1)
-            if before is not None:
-                ring_end(*before)
-            if q is not WIDE:
-                ring_step(q, t0, n, 2)
 
     keep = 2 - 2 * y_lo
 
     def deliver(half, to):
         return pltpu.make_async_remote_copy(
-            final.at[half, to], final_in.at[half, row], final_send.at[half], final_recv.at[half],
+            final.at[half, to], final_in.at[half, column], final_send.at[half], final_recv.at[half],
             device_id=(other, to), device_id_type=MESH,
         )
 
@@ -409,80 +428,103 @@
             final[half, a * 16 : a * 16 + 16] = jnp.concatenate(block).T.reshape(16, 8, HIGH)
 
     def dispatch(half):
-        for to in far_first:
+        for to, _ in far_first:
             deliver(half, to).start()
 
-    chunk(0, 0, 2, None, lambda: exchange_all(2, 4, 2))
+    chunk(0, 0, 2, lambda: exchange_all(2, 4, 2))
+
+    def second():
+        exchange_all(3, 6, 2)
+        apart(2)
+        apart(3)
+
+    chunk(1, 2, 2, second, (0, 0, 2))
 
     def middle(q, c):
         def ahead():
-            @pl.when(q == 3)
-            def _():
-                prepare_last()
-
             @pl.when(q < WIDE - 2)
             def _():
                 exchange_all(q + 2, 2 * q + 4, 2)
 
             @pl.when(q >= WIDE - 2)
             def _():
-                exchange_all(q + 2, q + 2 + WIDE, 1)
-
-        chunk(q, 2 * q, 2, (q - 1, 2 * q - 2, 2), ahead)
+                for j in range(2):
+                    i = 2 * (q + 2 - WIDE) + j
+                    exchange_all(WIDE + i, ALONE + i, 1)
+
+            @pl.when(q == 3)
+            def _():
+                prepare_alone()
+
+        chunk(q, 2 * q, 2, ahead, (q - 1, 2 * q - 2, 2), (q - 2, 2 * q - 4, 2))
         return c
 
-    lax.fori_loop(1, WIDE, middle, 0)
-    chunk(WIDE, 14, 1, (WIDE - 1, 12, 2), lambda: None)
-    with jax.named_scope("first_half"):
-        for q in range(4):
-            pair_copy(q, 2 * q, 2).wait_recv()
+    lax.fori_loop(2, WIDE, middle, 0)
+    def single(j):
+        with jax.named_scope("wait_alone"):
+            exchange_whole(WIDE + j, ALONE + j, 1).wait_recv()
+        if j == SINGLE - 1:
+            pair_copy(0).start()
+            pair_copy(1).start()
+        with jax.named_scope("C_alone"):
+            height_alone(j)
+
+    def summed(j):
+        for k in FAR:
+            from_z(sum_out.at[j], sum_in.at[j], sum_send.at[j], sum_recv.at[j], k).wait_recv()
+        lines = jnp.swapaxes(sum_in[j], 0, 1)
+        for k in range(2):
+            own[ALONE + j, :, k] = lines[4 * k : 4 * k + 4]
+
+    single(0)
+    with jax.named_scope("ring2"):
+        ring_end(WIDE - 2, ALONE - 4, 2)
+        ring_step(WIDE - 1, ALONE - 2, 2, 2)
+    single(1)
+    with jax.named_scope("ring3"):
+        ring_step(WIDE - 1, ALONE - 2, 2, 3)
+        summed(0)
+    single(2)
+    with jax.named_scope("ring_end"):
+        ring_end(WIDE - 1, ALONE - 2, 2)
+        summed(1)
+        summed(2)
+    single(3)
+    with jax.named_scope("pair0"):
+        pair_copy(0).wait_recv()
         hand_over(0)
-    with jax.named_scope("wait_last"):
-        exchange_whole(WIDE + 1, LAST, 1).wait_recv()
-    with jax.named_scope("C_last"):
-        height_last()
+    with jax.named_scope("sums"):
+        summed(3)
+        pair_copy(2).start()
+    dispatch(0)
+    with jax.named_scope("pair1"):
+        pair_copy(1).wait_recv()
+        pair_copy(2).wait_recv()
+    with jax.named_scope("pack1"):
+        hand_over(1)
+    dispatch(1)
+
+    def settle(q, c):
+        exchange_whole(q, 2 * q, 2).wait_send()
+        for step in range(7):
+            ring_copy(q, 2 * q, 2, step, z).wait_send()
+        return c
+
+    lax.fori_loop(0, WIDE, settle, 0)
+    for q in range(3):
+        pair_copy(q).wait_send()
+    for j in range(SINGLE):
+        exchange_whole(WIDE + j, ALONE + j, 1).wait_send()
+        for k in FAR:
+            along_z(z_out.at[j], z_in.at[j], z_send.at[j], z_recv.at[j], k).wait_send()
+            along_z(sum_out.at[j], sum_in.at[j], sum_send.at[j], sum_recv.at[j], k).wait_send()
     for k in FAR:
-        along_z(sum_out, sum_in, sum_send, sum_recv, k).start()
-    with jax.named_scope("last_ring"):
-        ring_step(WIDE, 14, 1, 2)
-        dispatch(0)
-        ring_step(WIDE, 14, 1, 3)
-    with jax.named_scope("last_sum"):
-        for k in FAR:
-            from_z(sum_out, sum_in, sum_send, sum_recv, k).wait_recv()
-        lines = jnp.swapaxes(sum_in[...], 0, 1)
-        for k in range(2):
-            own[LAST, :, k] = lines[4 * k : 4 * k + 4]
-        pair_copy(WIDE + 1, LAST, 1).start()
-        ring_end(WIDE, 14, 1)
-    with jax.named_scope("pair_wait"):
-        for q in range(4, WIDE):
-            pair_copy(q, 2 * q, 2).wait_recv()
-        for q in range(WIDE, CHUNKS):
-            pair_copy(q, q + WIDE, 1).wait_recv()
-    hand_over(1)
-    dispatch(1)
-
-    def settle(q, t0, n):
-        exchange_whole(q, t0, n).wait_send()
-        pair_copy(q, t0, n).wait_send()
-        if t0 is not LAST:
-            for step in range(7):
-                ring_copy(q, t0, n, step, z).wait_send()
-
-    lax.fori_loop(0, WIDE, lambda q, c: (settle(q, 2 * q, 2), c)[1], 0)
-    settle(WIDE, LAST - 1, 1)
-    settle(WIDE + 1, LAST, 1)
-    for k in FAR:
-        along_z(z_out, z_in, z_send, z_recv, k).wait_send()
         along_z(par_out, par_in, all_send, all_recv, k, True).wait_send()
-        along_z(sum_out, sum_in, sum_send, sum_recv, k).wait_send()
+    deliver_whole(0).wait_recv()
+    both = split_dot(final_in[0].reshape(8 * LOW, HIGH), w, 4, slice(0, HIGH))
     with jax.named_scope("final_wait"):
-        deliver_whole(0).wait_recv()
         deliver_whole(1).wait_recv()
-
-    left = jnp.concatenate([final_in[0].reshape(8 * LOW, HIGH), final_in[1].reshape(8 * LOW, HIGH)], axis=1)
-    both = split_dot(left, w, 4)
+    both = both + split_dot(final_in[1].reshape(8 * LOW, HIGH), w, 4, slice(HIGH, 2 * HIGH))
     re, im = both[:, :HIGH].reshape(LOW, 8, HIGH), both[:, HIGH:].reshape(LOW, 8, HIGH)
     cosine, sine = turn[0] * 0.25, turn[1] * 0.25
     pieces = dft32(re * cosine - im * sine, im * cosine + re * sine, small, 1)
@@ -501,7 +543,7 @@
     dma = pltpu.SemaphoreType.DMA
     return pl.pallas_call(
         kernel,
-        out_shape=jax.ShapeDtypeStruct((2, 8, N), F32),
+        out_shape=pltpu.VMEM((2, 8, N), F32),
         in_specs=[anywhere] * 8,
         out_specs=pl.BlockSpec(memory_space=pltpu.VMEM),
         scratch_shapes=[
@@ -511,7 +553,7 @@
             pltpu.VMEM((TILES, LOW, 2, 8, HIGH), F32),
             pltpu.VMEM((TILES, LOW, 2, 8, HIGH), F32),
             pltpu.VMEM((TILES, LOW, 2, 8, HIGH), F32),
-            pltpu.VMEM((TILES, 7, 4, 2, 8, HIGH), F32),
+            pltpu.VMEM((ALONE, 7, 4, 2, 8, HIGH), F32),
             pltpu.VMEM((TILES, 4, 2, 8, HIGH), F32),
             pltpu.VMEM((TILES, 2, 2, 8, HIGH), F32),
             pltpu.VMEM((2, LOW, 8, HIGH), F32),
@@ -525,30 +567,30 @@
             pltpu.VMEM(matrices.shape, BF16),
             pltpu.VMEM(flat.shape, F32),
             pltpu.VMEM(short.shape, BF16),
-            pltpu.VMEM((Z, 2 * LOW, HIGH), F32),
-            pltpu.VMEM((Z, 2 * LOW, HIGH), F32),
+            pltpu.VMEM((SINGLE, Z, 2 * LOW, HIGH), F32),
+            pltpu.VMEM((SINGLE, Z, 2 * LOW, HIGH), F32),
             pltpu.VMEM((8, HIGH), F32),
             pltpu.VMEM((Z, 8, HIGH), F32),
-            pltpu.VMEM((Z, 8, HIGH), F32),
-            pltpu.VMEM((Z, 8, HIGH), F32),
+            pltpu.VMEM((SINGLE, Z, 8, HIGH), F32),
+            pltpu.VMEM((SINGLE, Z, 8, HIGH), F32),
             dma((4,)),
             dma((6,)),
             dma((CHUNKS,)),
             dma((CHUNKS,)),
-            dma((CHUNKS, 7)),
-            dma((CHUNKS, 7)),
-            dma((CHUNKS,)),
-            dma((CHUNKS,)),
+            dma((WIDE, 7)),
+            dma((WIDE, 7)),
+            dma((3,)),
+            dma((3,)),
             dma((2,)),
             dma((2,)),
             dma((2,)),
             dma((2,)),
+            dma((SINGLE, Z)),
+            dma((SINGLE, Z)),
             dma((Z,)),
             dma((Z,)),
-            dma((Z,)),
-            dma((Z,)),
-            dma((Z,)),
-            dma((Z,)),
+            dma((SINGLE, Z)),
+            dma((SINGLE, Z)),
         ],
         compiler_params=pltpu.CompilerParams(
             collective_id=0, has_side_effects=True, vmem_limit_bytes=60 * 1024 * 1024

time: 140 us -> 132 us (0.943)
  Pallas kernels: 137 us -> 130 us
    pallas_call x1, Pallas kernels: 137 us -> 130 us  [local(): pl.pallas_call(kernel, out_shape=pltpu.VMEM((2, 8, N), F32), in_specs=[an...]
where the time goes in v3:
time: 132 us
  Pallas kernels  130 us (98%)
    pallas_call x1, Pallas kernels, local(): pl.pallas_call(kernel, out_shape=pltpu.VMEM((2, 8, N), F32), in_specs=[an...  130 us

profile of v3, /device:TPU:1, one launch (start us, length us, event | category | flops | bytes accessed | tf_op | source)
XLA Modules:
  0.0 131.7 jit_solution(11563155726028467835)
XLA Ops:
  0.7 130.3 %hologram.1 = f32[2,8,4096]{2,1,0:T(8,128)S(1)} custom-call(f32[1,2,128,4096]{3,2,1,0:T(8,128)} %x_ref.1, s32[1,2,4096]{2,1,0:T(2,128)} %mask_ref.1, s32[1]{0:T(128)S(6)} %copy.11.level_ref, f32[2,32,8,128]{3,2,1,0:T(8,128)} %constant.10.clone.turn_ref, f32[2,3,8,8,128]{4,3,2,1,0:T(8,128)} %constant.11.clone.small_ref, ...), custom_call_target="tpu_custom_call" | custom-call | tf_op jit(solution)/shard_map/hologram/pallas_call | solution.py:544
  131.0 0.7 copy.10

commit v4 on v3

--- a/solution.py
+++ b/solution.py
@@ -20,7 +20,7 @@
 SINGLE = 4
 CHUNKS = WIDE + SINGLE
 ALONE = 2 * WIDE
-PAIRED = (0, 8, 15, 16)
+PAIRED = (0, 8, 15)
 FAR = (4, 3, 5, 2, 6, 1, 7)
 F32 = jnp.float32
 BF16 = jnp.bfloat16
@@ -104,9 +104,9 @@
 def kernel(
     x_ref, mask_ref, level_ref, turn_ref, small_ref, w_ref, flat_ref, short_ref, out_ref,
     xbuf, tbuf, send, recv, prop, part, ring, own, pair, final, final_in, mask_in, level_at, level_out, level_in,
-    turn, small, w, flat, short, z_out, z_in, par_out, par_in, sum_out, sum_in,
+    turn, small, w, flat, short, z_out, z_in, par_out, par_in, sum_out, sum_in, mate_in, mate_own,
     x_sem, in_sem, send_sem, recv_sem, ring_send, ring_recv, pair_send, pair_recv, final_send, final_recv,
-    par_send, par_recv, z_send, z_recv, all_send, all_recv, sum_send, sum_recv,
+    par_send, par_recv, z_send, z_recv, all_send, all_recv, sum_send, sum_recv, mate_send, mate_recv,
 ):
     depth = lax.axis_index("depth")
     row = lax.axis_index("rows")
@@ -156,13 +156,11 @@
 
     barrier = pltpu.get_barrier_semaphore()
 
-    def greet(i, c):
-        pl.semaphore_signal(barrier, inc=1, device_id=(other, i), device_id_type=MESH)
-        return c
-
-    lax.fori_loop(0, 32, greet, 0)
-    for k in FAR:
-        pl.semaphore_signal(barrier, inc=1, device_id=(2 * lax.rem(z + k, Z) + y_lo, row), device_id_type=MESH)
+    with jax.named_scope("greet"):
+        for to in [(other, r) for r, _ in far_first] + [(2 * lax.rem(z + k, Z) + y_lo, row) for k in FAR] + [
+            (2 * lax.rem(z + k, Z) + 1 - y_lo, mate) for k in FAR
+        ]:
+            pl.semaphore_signal(barrier, inc=1, device_id=to, device_id_type=MESH)
 
     load_small.wait()
     load_turn.wait()
@@ -189,7 +187,7 @@
     load_flat.wait()
     load_short.wait()
     with jax.named_scope("barrier"):
-        pl.semaphore_wait(barrier, 39)
+        pl.semaphore_wait(barrier, 46)
     mask_copy = pltpu.make_async_remote_copy(
         mask_ref, mask_in, par_send.at[0], par_recv.at[0], device_id=(other, row), device_id_type=MESH
     )
@@ -202,14 +200,14 @@
     def exchange(q, t0, n, to, block):
         tiles = pl.ds(t0, n)
         return pltpu.make_async_remote_copy(
-            send.at[tiles, block], recv.at[tiles, row], send_sem.at[q], recv_sem.at[q],
+            send.at[tiles, block], recv.at[tiles, row], send_sem, recv_sem.at[q],
             device_id=(other, to), device_id_type=MESH,
         )
 
     def exchange_whole(q, t0, n):
         tiles = pl.ds(t0, n)
         return pltpu.make_async_remote_copy(
-            send.at[tiles], recv.at[tiles], send_sem.at[q], recv_sem.at[q],
+            send.at[tiles], recv.at[tiles], send_sem, recv_sem.at[q],
             device_id=(other, row), device_id_type=MESH,
         )
 
@@ -217,19 +215,22 @@
         for to, block in near_first:
             exchange(q, t0, n, to, block).start()
 
-    def along_z(out, into, send_sems, recv_sems, k, shared=False):
+    def along_z(out, into, send_sem, recv_sem, k, shared=False):
         to = lax.rem(z + k, Z)
         return pltpu.make_async_remote_copy(
-            out if shared else out.at[to], into.at[z], send_sems.at[k], recv_sems.at[z],
+            out if shared else out.at[to], into.at[z], send_sem, recv_sem,
             device_id=(2 * to + y_lo, row), device_id_type=MESH,
         )
 
-    def from_z(out, into, send_sems, recv_sems, k, shared=False):
-        source = lax.rem(z + k, Z)
-        return pltpu.make_async_remote_copy(
-            out if shared else out.at[source], into.at[source], send_sems.at[k], recv_sems.at[source],
-            device_id=(2 * source + y_lo, row), device_id_type=MESH,
-        )
+    def amount(buffer, send_sem, recv_sem):
+        return pltpu.make_async_remote_copy(
+            buffer, buffer, send_sem, recv_sem, device_id=(other, row), device_id_type=MESH
+        )
+
+    seven = pl.ds(0, Z - 1)
+    all_z = amount(z_in.at[:, seven], z_send, z_recv)
+    all_par = amount(par_in.at[seven], all_send, all_recv)
+    all_mate = amount(mate_in, mate_send, mate_recv)
 
     def width_last(g, c):
         @pl.when(g > 0)
@@ -253,7 +254,7 @@
     lax.fori_loop(28, 32, lambda i, c: (exchange(0, 0, 2, *peer(i)).start(), c)[1], 0)
     def apart(j):
         for k in FAR:
-            along_z(z_out.at[j], z_in.at[j], z_send.at[j], z_recv.at[j], k).start()
+            along_z(z_out.at[j], z_in.at[j], z_send, z_recv, k).start()
         z_in[j, z] = z_out[j, z]
 
     apart(0)
@@ -309,10 +310,8 @@
         along_z(par_out, par_in, all_send, all_recv, k, True).start()
 
     def prepare_alone():
-        for k in FAR:
-            for j in range(SINGLE):
-                from_z(z_out.at[j], z_in.at[j], z_send.at[j], z_recv.at[j], k).wait_recv()
-            from_z(par_out, par_in, all_send, all_recv, k, True).wait_recv()
+        all_z.wait_recv()
+        all_par.wait_recv()
         for j in range(SINGLE):
             for g in range(8):
                 block = jnp.swapaxes(z_in[j, :, 8 * g : 8 * g + 8, :], 0, 1)
@@ -338,6 +337,13 @@
         part[t, :, 1] = im
         return c
 
+    def to_mate(k):
+        to = lax.rem(z + k, Z)
+        return pltpu.make_async_remote_copy(
+            sum_out.at[SINGLE - 1, to], mate_in.at[z], mate_send, mate_recv,
+            device_id=(2 * to + 1 - y_lo, mate), device_id_type=MESH,
+        )
+
     def height_alone(j):
         t = ALONE + j
         re, im = joined(dft32(recv[t, :, 0], recv[t, :, 1], small, -1))
@@ -357,22 +363,31 @@
         result = dot(short[0], top) + (dot(short[0], rest) + dot(short[1], top))
         sum_out[j] = result.reshape(Z, 8, HIGH)
         sum_in[j, z] = sum_out[j, z]
+        if j == SINGLE - 1:
+            for k in FAR + (0,):
+                to_mate(k).start()
         for k in FAR:
-            along_z(sum_out.at[j], sum_in.at[j], sum_send.at[j], sum_recv.at[j], k).start()
+            along_z(sum_out.at[j], sum_in.at[j], sum_send, sum_recv.at[j], k).start()
 
     def ring_copy(q, t0, n, step, source):
         tiles = pl.ds(t0, n)
         return pltpu.make_async_remote_copy(
-            part.at[tiles, pl.ds(source * 4, 4)], ring.at[tiles, step], ring_send.at[q, step], ring_recv.at[q, step],
+            part.at[tiles, pl.ds(source * 4, 4)], ring.at[tiles, step], ring_send,
+            ring_recv.at[q, {4: 0, 5: 1, 6: 3}.get(step, step)],
             device_id=(up if step < 4 else down, row), device_id_type=MESH,
         )
+
+    def ring_wait(q, t0, n, step):
+        blocks = ring.at[pl.ds(t0, n), pl.ds(0, 1 if step == 2 else 2)]
+        amount(blocks, ring_send, ring_recv.at[q, step]).wait_recv()
 
     def ring_step(q, t0, n, step):
         tiles = pl.ds(t0, n)
         lines = [(step, lax.rem(z + 4 - step, Z))] + ([(step + 4, lax.rem(z + 5 + step, Z))] if step < 3 else [])
+        if step > 0:
+            ring_wait(q, t0, n, step - 1)
         for i, source in lines:
             if step > 0:
-                ring_copy(q, t0, n, i - 1, source).wait_recv()
                 block = pl.ds(source * 4, 4)
                 part[tiles, block] = part[tiles, block] + ring[tiles, i - 1]
         for i, source in lines:
@@ -387,8 +402,7 @@
 
     def ring_end(q, t0, n):
         tiles = pl.ds(t0, n)
-        ring_copy(q, t0, n, 6, z).wait_recv()
-        ring_copy(q, t0, n, 3, z).wait_recv()
+        ring_wait(q, t0, n, 3)
         own[tiles] = part[tiles, pl.ds(z * 4, 4)] + (ring[tiles, 3] + ring[tiles, 6])
 
     def chunk(q, t0, n, ahead, before=None, ended=None):
@@ -411,13 +425,13 @@
 
     def deliver(half, to):
         return pltpu.make_async_remote_copy(
-            final.at[half, to], final_in.at[half, column], final_send.at[half], final_recv.at[half],
+            final.at[half, to], final_in.at[half, column], final_send, final_recv.at[half],
             device_id=(other, to), device_id_type=MESH,
         )
 
     def deliver_whole(half):
         return pltpu.make_async_remote_copy(
-            final.at[half], final_in.at[half], final_send.at[half], final_recv.at[half],
+            final.at[half], final_in.at[half], final_send, final_recv.at[half],
             device_id=(other, row), device_id_type=MESH,
         )
 
@@ -463,15 +477,13 @@
     def single(j):
         with jax.named_scope("wait_alone"):
             exchange_whole(WIDE + j, ALONE + j, 1).wait_recv()
-        if j == SINGLE - 1:
+        if j == SINGLE - 2:
             pair_copy(0).start()
-            pair_copy(1).start()
         with jax.named_scope("C_alone"):
             height_alone(j)
 
     def summed(j):
-        for k in FAR:
-            from_z(sum_out.at[j], sum_in.at[j], sum_send.at[j], sum_recv.at[j], k).wait_recv()
+        amount(sum_in.at[j, seven], sum_send, sum_recv.at[j]).wait_recv()
         lines = jnp.swapaxes(sum_in[j], 0, 1)
         for k in range(2):
             own[ALONE + j, :, k] = lines[4 * k : 4 * k + 4]
@@ -488,39 +500,38 @@
     with jax.named_scope("ring_end"):
         ring_end(WIDE - 1, ALONE - 2, 2)
         summed(1)
-        summed(2)
-    single(3)
     with jax.named_scope("pair0"):
         pair_copy(0).wait_recv()
         hand_over(0)
+    single(3)
+    with jax.named_scope("dispatch0"):
+        summed(2)
+        pair_copy(1).start()
+        dispatch(0)
     with jax.named_scope("sums"):
-        summed(3)
-        pair_copy(2).start()
-    dispatch(0)
+        summed(SINGLE - 1)
+        all_mate.wait_recv()
+        lines = jnp.swapaxes(mate_in[...], 0, 1)
+        for k in range(2):
+            mate_own[:, k] = lines[4 * k : 4 * k + 4]
+        pair[TILES - 1] = mate_own[pl.ds(keep, 2)]
     with jax.named_scope("pair1"):
         pair_copy(1).wait_recv()
-        pair_copy(2).wait_recv()
     with jax.named_scope("pack1"):
         hand_over(1)
-    dispatch(1)
-
-    def settle(q, c):
-        exchange_whole(q, 2 * q, 2).wait_send()
-        for step in range(7):
-            ring_copy(q, 2 * q, 2, step, z).wait_send()
-        return c
-
-    lax.fori_loop(0, WIDE, settle, 0)
-    for q in range(3):
+    with jax.named_scope("dispatch1"):
+        dispatch(1)
+
+    amount(send, send_sem, recv_sem.at[0]).wait_send()
+    amount(ring, ring_send, ring_recv.at[0, 0]).wait_send()
+    for q in range(2):
         pair_copy(q).wait_send()
-    for j in range(SINGLE):
-        exchange_whole(WIDE + j, ALONE + j, 1).wait_send()
-        for k in FAR:
-            along_z(z_out.at[j], z_in.at[j], z_send.at[j], z_recv.at[j], k).wait_send()
-            along_z(sum_out.at[j], sum_in.at[j], sum_send.at[j], sum_recv.at[j], k).wait_send()
-    for k in FAR:
-        along_z(par_out, par_in, all_send, all_recv, k, True).wait_send()
-    deliver_whole(0).wait_recv()
+    all_z.wait_send()
+    all_par.wait_send()
+    all_mate.wait_send()
+    amount(sum_in.at[:, seven], sum_send, sum_recv.at[0]).wait_send()
+    with jax.named_scope('final_wait0'):
+        deliver_whole(0).wait_recv()
     both = split_dot(final_in[0].reshape(8 * LOW, HIGH), w, 4, slice(0, HIGH))
     with jax.named_scope("final_wait"):
         deliver_whole(1).wait_recv()
@@ -533,8 +544,8 @@
             lanes = pl.ds((k * 4 + j) * HIGH, HIGH)
             out_ref[0, :, lanes] = pieces[k][0][j]
             out_ref[1, :, lanes] = pieces[k][1][j]
-    deliver_whole(0).wait_send()
-    deliver_whole(1).wait_send()
+    with jax.named_scope("last_sends"):
+        amount(final, final_send, final_recv.at[0]).wait_send()
 
 
 def local(target, depth_index, band_mask):
@@ -544,7 +555,7 @@
     return pl.pallas_call(
         kernel,
         out_shape=pltpu.VMEM((2, 8, N), F32),
-        in_specs=[anywhere] * 8,
+        in_specs=[anywhere] * 2 + [pl.BlockSpec(memory_space=pltpu.HBM)] + [anywhere] * 5,
         out_specs=pl.BlockSpec(memory_space=pltpu.VMEM),
         scratch_shapes=[
             pltpu.VMEM((2, HIGH, N), F32),
@@ -573,24 +584,28 @@
             pltpu.VMEM((Z, 8, HIGH), F32),
             pltpu.VMEM((SINGLE, Z, 8, HIGH), F32),
             pltpu.VMEM((SINGLE, Z, 8, HIGH), F32),
+            pltpu.VMEM((Z, 8, HIGH), F32),
+            pltpu.VMEM((4, 2, 8, HIGH), F32),
             dma((4,)),
             dma((6,)),
+            dma,
             dma((CHUNKS,)),
-            dma((CHUNKS,)),
-            dma((WIDE, 7)),
-            dma((WIDE, 7)),
-            dma((3,)),
-            dma((3,)),
+            dma,
+            dma((WIDE, 4)),
+            dma((2,)),
+            dma((2,)),
+            dma,
             dma((2,)),
             dma((2,)),
             dma((2,)),
-            dma((2,)),
-            dma((SINGLE, Z)),
-            dma((SINGLE, Z)),
-            dma((Z,)),
-            dma((Z,)),
-            dma((SINGLE, Z)),
-            dma((SINGLE, Z)),
+            dma,
+            dma,
+            dma,
+            dma,
+            dma,
+            dma((SINGLE,)),
+            dma,
+            dma,
         ],
         compiler_params=pltpu.CompilerParams(
             collective_id=0, has_side_effects=True, vmem_limit_bytes=60 * 1024 * 1024

time: 132 us -> 127 us (0.962)
  Pallas kernels: 130 us -> 125 us
    pallas_call x1, Pallas kernels: 130 us -> 125 us  [local(): pl.pallas_call(kernel, out_shape=pltpu.VMEM((2, 8, N), F32), in_specs=[an...]
where the time goes in v4:
time: 127 us; the launch traced here: 126 us
  Pallas kernels  125 us (98%)
    pallas_call x1, Pallas kernels, local(): pl.pallas_call(kernel, out_shape=pltpu.VMEM((2, 8, N), F32), in_specs=[an...  125 us

profile of v4, /device:TPU:1, one launch (start us, length us, event | category | flops | bytes accessed | tf_op | source)
XLA Modules:
  0.0 126.4 jit_solution(15042357451327341928)
XLA Ops:
  0.7 125.1 %hologram.1 = f32[2,8,4096]{2,1,0:T(8,128)S(1)} custom-call(f32[1,2,128,4096]{3,2,1,0:T(8,128)} %x_ref.1, s32[1,2,4096]{2,1,0:T(2,128)} %mask_ref.1, s32[1]{0:T(128)S(6)} %copy.11.level_ref, f32[2,32,8,128]{3,2,1,0:T(8,128)} %constant.10.clone.turn_ref, f32[2,3,8,8,128]{4,3,2,1,0:T(8,128)} %constant.11.clone.small_ref, ...), custom_call_target="tpu_custom_call" | custom-call | tf_op jit(solution)/shard_map/hologram/pallas_call | solution.py:555
  125.7 0.7 copy.10

commit v5 on v4

--- a/solution.py
+++ b/solution.py
@@ -61,17 +61,17 @@
     return [(s0r + s1r, s0i + s1i), first, (s0r - s1r, s0i - s1i), third]
 
 
-def dft32(re, im, small_ref, sign):
+def turned4(columns, small_ref, part, sign):
+    turned = dft4(columns, sign)
+    for k in range(1, 4):
+        r, i = turned[k]
+        c, s = small_ref[0, k - 1, part], small_ref[1, k - 1, part]
+        turned[k] = (r * c + i * s, i * c - r * s) if sign < 0 else (r * c - i * s, i * c + r * s)
+    return turned
+
+
+def dft8(rows, sign):
     half = math.sqrt(0.5)
-    columns = dft4([(re[8 * n : 8 * n + 8], im[8 * n : 8 * n + 8]) for n in range(4)], sign)
-    turned = [columns[0]]
-    for k in range(1, 4):
-        r, i = columns[k]
-        c, s = small_ref[0, k - 1], small_ref[1, k - 1]
-        turned.append((r * c + i * s, i * c - r * s) if sign < 0 else (r * c - i * s, i * c + r * s))
-    re = jnp.stack([t[0] for t in turned])
-    im = jnp.stack([t[1] for t in turned])
-    rows = [(re[:, n], im[:, n]) for n in range(8)]
     even = dft4(rows[0::2], sign)
     odd = dft4(rows[1::2], sign)
     (r1, i1), (r2, i2), (r3, i3) = odd[1:]
@@ -83,6 +83,14 @@
     return result + [(e[0] - o[0], e[1] - o[1]) for e, o in zip(even, odd)]
 
 
+def dft32(re, im, small_ref, sign):
+    columns = [(re[8 * n : 8 * n + 8], im[8 * n : 8 * n + 8]) for n in range(4)]
+    turned = turned4(columns, small_ref, slice(None), sign)
+    re = jnp.stack([t[0] for t in turned])
+    im = jnp.stack([t[1] for t in turned])
+    return dft8([(re[:, n], im[:, n]) for n in range(8)], sign)
+
+
 def joined(pieces):
     return jnp.concatenate([p[0] for p in pieces]), jnp.concatenate([p[1] for p in pieces])
 
@@ -104,7 +112,7 @@
 def kernel(
     x_ref, mask_ref, level_ref, turn_ref, small_ref, w_ref, flat_ref, short_ref, out_ref,
     xbuf, tbuf, send, recv, prop, part, ring, own, pair, final, final_in, mask_in, level_at, level_out, level_in,
-    turn, small, w, flat, short, z_out, z_in, par_out, par_in, sum_out, sum_in, mate_in, mate_own,
+    turn, small, w, flat, short, z_out, z_in, par_out, par_in, sum_out, sum_in, mate_in, mate_own, stage,
     x_sem, in_sem, send_sem, recv_sem, ring_send, ring_recv, pair_send, pair_recv, final_send, final_recv,
     par_send, par_recv, z_send, z_recv, all_send, all_recv, sum_send, sum_recv, mate_send, mate_recv,
 ):
@@ -167,16 +175,27 @@
 
     def width_first(t, c):
         rows = pl.ds(pl.multiple_of(t * 8, 8), 8)
-        cells = [jnp.stack([xbuf[k, rows, a * HIGH : (a + 1) * HIGH] for a in range(LOW)]) for k in range(2)]
-        re, im = joined(dft32(cells[0], cells[1], small, -1))
-        cosine, sine = turn[0], turn[1]
-        tbuf[:, 0, rows, :] = re * cosine + im * sine
-        tbuf[:, 1, rows, :] = im * cosine - re * sine
+        for m in range(0, 8, 2):
+            columns = [
+                tuple(jnp.stack([xbuf[k, rows, a * HIGH : (a + 1) * HIGH] for a in (8 * n + m, 8 * n + m + 1)]) for k in range(2))
+                for n in range(4)
+            ]
+            for k, (r, i) in enumerate(turned4(columns, small, slice(m, m + 2), -1)):
+                stage[0, m : m + 2, k] = r
+                stage[1, m : m + 2, k] = i
+        for k in range(0, 4, 2):
+            pieces = dft8([(stage[0, n, k : k + 2], stage[1, n, k : k + 2]) for n in range(8)], -1)
+            for n in range(8):
+                re, im = pieces[n]
+                to = slice(4 * n + k, 4 * n + k + 2)
+                cosine, sine = turn[0, to], turn[1, to]
+                tbuf[to, 0, rows, :] = re * cosine + im * sine
+                tbuf[to, 1, rows, :] = im * cosine - re * sine
         return c
 
     def width_group(g, c):
         load(g).wait()
-        return lax.fori_loop(g * 4, g * 4 + 4, width_first, c)
+        return lax.fori_loop(0, 4, lambda t, c: width_first(g * 4 + t, c), c)
 
     with jax.named_scope("A1"):
         lax.fori_loop(0, 4, width_group, 0)
@@ -212,7 +231,7 @@
         )
 
     def exchange_all(q, t0, n):
-        for to, block in near_first:
+        for to, block in near_first if n > 1 else far_first:
             exchange(q, t0, n, to, block).start()
 
     def along_z(out, into, send_sem, recv_sem, k, shared=False):
@@ -500,13 +519,13 @@
     with jax.named_scope("ring_end"):
         ring_end(WIDE - 1, ALONE - 2, 2)
         summed(1)
+    single(3)
     with jax.named_scope("pair0"):
+        summed(2)
+        pair_copy(1).start()
         pair_copy(0).wait_recv()
         hand_over(0)
-    single(3)
     with jax.named_scope("dispatch0"):
-        summed(2)
-        pair_copy(1).start()
         dispatch(0)
     with jax.named_scope("sums"):
         summed(SINGLE - 1)
@@ -586,6 +605,7 @@
             pltpu.VMEM((SINGLE, Z, 8, HIGH), F32),
             pltpu.VMEM((Z, 8, HIGH), F32),
             pltpu.VMEM((4, 2, 8, HIGH), F32),
+            pltpu.VMEM((2, 8, 4, 8, HIGH), F32),
             dma((4,)),
             dma((6,)),
             dma,

time: 127 us -> 126 us (level)
  no operation moved by 1% of the time
where the time goes in v5:
time: 126 us
  Pallas kernels  125 us (99%)
    pallas_call x1, Pallas kernels, local(): pl.pallas_call(kernel, out_shape=pltpu.VMEM((2, 8, N), F32), in_specs=[an...  125 us

profile of v5, /device:TPU:1, one launch (start us, length us, event | category | flops | bytes accessed | tf_op | source)
XLA Modules:
  0.0 125.9 jit_solution(9277135801653420402)
XLA Ops:
  0.7 124.5 %hologram.1 = f32[2,8,4096]{2,1,0:T(8,128)S(1)} custom-call(f32[1,2,128,4096]{3,2,1,0:T(8,128)} %x_ref.1, s32[1,2,4096]{2,1,0:T(2,128)} %mask_ref.1, s32[1]{0:T(128)S(6)} %copy.11.level_ref, f32[2,32,8,128]{3,2,1,0:T(8,128)} %constant.10.clone.turn_ref, f32[2,3,8,8,128]{4,3,2,1,0:T(8,128)} %constant.11.clone.small_ref, ...), custom_call_target="tpu_custom_call" | custom-call | tf_op jit(solution)/shard_map/hologram/pallas_call | solution.py:574
  125.2 0.7 copy.10

commit v6 on v5

--- a/solution.py
+++ b/solution.py
@@ -157,6 +157,8 @@
         load(g).start()
     load_w.start()
     load_level.start()
+    load_mask = pltpu.make_async_copy(mask_ref, mask_in, in_sem.at[6])
+    load_mask.start()
     load_flat = pltpu.make_async_copy(flat_ref, flat, in_sem.at[4])
     load_short = pltpu.make_async_copy(short_ref, short, in_sem.at[5])
     load_flat.start()
@@ -201,19 +203,23 @@
         lax.fori_loop(0, 4, width_group, 0)
 
     load_level.wait()
-    level_out[...] = jnp.full((8, HIGH), level_at[0].astype(F32))
+    load_mask.wait()
+
+    def cutoff(k):
+        total = jnp.sum(mask_in[0, k : k + 1, :].astype(F32), axis=1, keepdims=True)
+        return jnp.broadcast_to((total + 1.0) * 0.5, (8, HIGH))
+
+    line = lax.broadcasted_iota(jnp.int32, (8, HIGH), 0)
+    level = jnp.full((8, HIGH), 100.0 + 2.0 * level_at[0].astype(F32))
+    level_out[...] = jnp.where(line == 0, level, jnp.where(line == 1, cutoff(0), cutoff(1)))
     load_w.wait()
     load_flat.wait()
     load_short.wait()
     with jax.named_scope("barrier"):
         pl.semaphore_wait(barrier, 46)
-    mask_copy = pltpu.make_async_remote_copy(
-        mask_ref, mask_in, par_send.at[0], par_recv.at[0], device_id=(other, row), device_id_type=MESH
+    level_copy = pltpu.make_async_remote_copy(
+        level_out, level_in, par_send, par_recv, device_id=(other, row), device_id_type=MESH
     )
-    level_copy = pltpu.make_async_remote_copy(
-        level_out, level_in, par_send.at[1], par_recv.at[1], device_id=(other, row), device_id_type=MESH
-    )
-    mask_copy.start()
     level_copy.start()
 
     def exchange(q, t0, n, to, block):
@@ -280,19 +286,10 @@
     apart(1)
     exchange_all(1, 2, 2)
 
-    mask_copy.wait()
     level_copy.wait()
-    distance = 100.0 + 2.0 * level_in[...]
-
-    def cutoff(k):
-        total = jnp.sum(mask_in[0, k : k + 1, :].astype(F32), axis=1, keepdims=True)
-        return jnp.broadcast_to((total + 1.0) * 0.5, (8, HIGH))
-
-    cut_y, cut_x = cutoff(0), cutoff(1)
-    line = lax.broadcasted_iota(jnp.int32, (8, HIGH), 0)
-    about = jnp.where(line == 0, distance, jnp.where(line == 1, cut_y, cut_x))
-    par_out[...] = about
-    par_in[z] = about
+    distance, cut_y, cut_x = [jnp.broadcast_to(level_in[j : j + 1, :], (8, HIGH)) for j in range(3)]
+    par_out[...] = level_in[...]
+    par_in[z] = level_in[...]
     shape = (8, 8, HIGH)
 
     def signed(k):
@@ -607,7 +604,7 @@
             pltpu.VMEM((4, 2, 8, HIGH), F32),
             pltpu.VMEM((2, 8, 4, 8, HIGH), F32),
             dma((4,)),
-            dma((6,)),
+            dma((7,)),
             dma,
             dma((CHUNKS,)),
             dma,
@@ -616,8 +613,8 @@
             dma((2,)),
             dma,
             dma((2,)),
-            dma((2,)),
-            dma((2,)),
+            dma,
+            dma,
             dma,
             dma,
             dma,

time: 126 us -> 125 us (level)
  no operation moved by 1% of the time
where the time goes in v6:
time: 125 us
  Pallas kernels  124 us (99%)
    pallas_call x1, Pallas kernels, local(): pl.pallas_call(kernel, out_shape=pltpu.VMEM((2, 8, N), F32), in_specs=[an...  124 us

profile of v6, /device:TPU:1, one launch (start us, length us, event | category | flops | bytes accessed | tf_op | source)
XLA Modules:
  0.0 125.1 jit_solution(13400559387384143106)
XLA Ops:
  0.7 123.8 %hologram.1 = f32[2,8,4096]{2,1,0:T(8,128)S(1)} custom-call(f32[1,2,128,4096]{3,2,1,0:T(8,128)} %x_ref.1, s32[1,2,4096]{2,1,0:T(2,128)} %mask_ref.1, s32[1]{0:T(128)S(6)} %copy.11.level_ref, f32[2,32,8,128]{3,2,1,0:T(8,128)} %constant.10.clone.turn_ref, f32[2,3,8,8,128]{4,3,2,1,0:T(8,128)} %constant.11.clone.small_ref, ...), custom_call_target="tpu_custom_call" | custom-call | tf_op jit(solution)/shard_map/hologram/pallas_call | solution.py:571
  124.4 0.7 copy.10
